TPU v7x, 128 devices: a whole 4x4x4 slice. The times are simulated.
128 devices in a mesh: dp: 32 (over z, x_lo, y), mp: 4 (over x_hi, core).
Axes of the slice: x: 4 (x_hi: 2, x_lo: 2; x = x_hi * 2 + x_lo), y: 4, z: 4, core: 2. Of those that a mesh axis runs over, the one named last changes fastest.
Arguments:
- series: bfloat16 [32768, 1280], P('dp'), may hold values from -6 to 6
- inner_weight: bfloat16 [1280, 1280], P('mp'), may hold values from -0.15625 to 0.15625
- inner_bias: float32 [1280], P('mp'), may hold values from -3 to 3
- outer_weight: bfloat16 [1280, 1280], P('mp'), may hold values from -0.15625 to 0.15625
- skip_weight: bfloat16 [1280, 1280], P('mp'), may hold values from -0.15625 to 0.15625
- outer_bias: float32 [1280], replicated, may hold values from -3 to 3
- targets: float32 [32768, 128], P('dp'), may hold values from -9 to 9
- levels: int32 [10], replicated, may hold values from 0 to 8
- counts: int32 [2048], P('dp'), may hold values from 1 to 16
Outputs:
- input_grad: float32 [32768, 1280], P('dp', 'mp')
- inner_grad: float32 [1280, 1280], P(('mp', 'dp'))
- outer_grad: float32 [1280, 1280], P(('mp', 'dp'))
- skip_grad: float32 [1280, 1280], P(('mp', 'dp'))
- inbias_grad: float32 [1280], P(('mp', 'dp'))
- outbias_grad: float32 [1280], P('dp')
All inputs are finite; a program needn't handle non-finite values.
Results may differ from a plain program's by a relative error of at most 0.0039.
Values may be sent and summed in bfloat16 or wider, within the bound.
A program may use at most 64 MiB of HBM per device.

v0:
```python
import jax
import jax.numpy as jnp
from jax import lax
from jax.sharding import PartitionSpec as P

LEVELS = 9


huber_width = 0.5


def laid_out(tiles, dim):
    tiles = jnp.moveaxis(tiles, 0, dim)
    dims = tiles.shape
    return tiles.reshape(*dims[:dim], dims[dim] * dims[dim + 1], *dims[dim + 2 :])


def copy_for_each(array, axis):
    copies = jnp.broadcast_to(array, (lax.axis_size(axis), *array.shape))
    return lax.all_to_all(copies, axis, split_axis=0, concat_axis=0, tiled=True)


def collect(array, axis, dim):
    return laid_out(copy_for_each(array, axis), dim)


def in_blocks(array, dim, length):
    before, after = (array.shape[:dim], array.shape[dim + 1 :])
    return jnp.moveaxis(array.reshape(*before, length, -1, *after), dim, 0)


def sum_packed(arrays, axis, dims):
    length = lax.axis_size(axis)
    tiles = [in_blocks(a, dim, length) for a, dim in zip(arrays, dims)]
    lines = jnp.concatenate([b.reshape(length, -1) for b in tiles], axis=1)
    span = max(16, -(-lines.shape[1] // 1024) * 8)
    lines = jnp.pad(lines, ((0, 0), (0, span * 128 - lines.shape[1]))).reshape(-1, 128)
    flat, at, gathered = (lax.psum_scatter(lines, axis, tiled=True).reshape(-1), 0, [])
    for b in tiles:
        part = b[0]
        gathered.append(flat[at : at + part.size].reshape(part.shape))
        at += part.size
    return tuple(gathered)


def output_slope(predicted, target_rows, count_rows, levels):
    row_count = predicted.shape[0]
    window_count = count_rows.shape[0]
    patch_count = row_count // window_count
    horizon = target_rows.shape[1]
    quantiles = levels.shape[0]
    fraction = (levels.astype(jnp.float32) + 1.0) / (LEVELS + 1)
    level_cols = jnp.broadcast_to(fraction[None, :], (horizon, quantiles)).reshape(
        horizon * quantiles
    )
    spread = jnp.broadcast_to(target_rows[:, :, None], (row_count, horizon, quantiles)).reshape(
        row_count, horizon * quantiles
    )
    residue = spread - predicted
    slopes = jnp.where(residue >= 0, level_cols, 1.0 - level_cols) * jnp.clip(
        residue / huber_width, -1.0, 1.0
    )
    positions = lax.broadcasted_iota(jnp.int32, (window_count, patch_count), 1)
    validity = (positions < count_rows[:, None]).astype(jnp.float32)
    weights = (validity / count_rows[:, None].astype(jnp.float32)).reshape(row_count, 1)
    return (-slopes * weights).astype(jnp.bfloat16)


def on_device(
    series, inner_weight, inner_bias, outer_weight, skip_weight, outer_bias, targets, levels, counts
):
    row_count = series.shape[0]
    window_count = counts.shape[0]
    slice_width = skip_weight.shape[0]
    model_index = lax.axis_index("mp")
    model_size = lax.axis_size("mp")
    on_last = (((1,), (1,)), ((), ()))
    over_rows = (((0,), (0,)), ((), ()))
    own_series = lax.dynamic_slice_in_dim(series, model_index * slice_width, slice_width, 1)
    preact = (
        lax.dot_general(series, inner_weight, on_last, preferred_element_type=jnp.float32)
        + inner_bias
    )
    sigmoids = jax.nn.sigmoid(preact)
    hidden = (preact * sigmoids).astype(jnp.bfloat16)
    partial_out = jnp.dot(hidden, outer_weight, preferred_element_type=jnp.float32) + jnp.dot(
        own_series, skip_weight, preferred_element_type=jnp.float32
    )
    share_rows = row_count // model_size
    share_windows = window_count // model_size
    predicted = lax.psum_scatter(partial_out, "mp", scatter_dimension=0, tiled=True) + outer_bias
    target_share = lax.dynamic_slice_in_dim(targets, model_index * share_rows, share_rows, 0)
    count_share = lax.dynamic_slice_in_dim(counts, model_index * share_windows, share_windows, 0)
    out_grad = collect(output_slope(predicted, target_share, count_share, levels), "mp", 0)
    backflow = lax.dot_general(out_grad, outer_weight, on_last, preferred_element_type=jnp.float32)
    hidden_grad = (backflow * sigmoids * (1.0 + preact * (1.0 - sigmoids))).astype(jnp.bfloat16)
    skip_part = lax.dot_general(out_grad, skip_weight, on_last, preferred_element_type=jnp.float32)
    columns = lax.all_to_all(inner_weight, "mp", split_axis=1, concat_axis=0, tiled=True)
    input_total = skip_part + jnp.dot(
        lax.all_gather(hidden_grad, "mp", axis=1, tiled=True),
        columns,
        preferred_element_type=jnp.float32,
    )
    inner_part = lax.dot_general(hidden_grad, series, over_rows, preferred_element_type=jnp.float32)
    outer_part = lax.dot_general(hidden, out_grad, over_rows, preferred_element_type=jnp.float32)
    skip_grad_part = lax.dot_general(
        own_series, out_grad, over_rows, preferred_element_type=jnp.float32
    )
    inbias_part = jnp.sum(hidden_grad, axis=0, dtype=jnp.float32)
    outbias_part = jnp.sum(out_grad, axis=0, dtype=jnp.float32)
    summed = sum_packed(
        (inner_part, outer_part, skip_grad_part, inbias_part, outbias_part), "dp", (0, 0, 0, 0, 0)
    )
    rescale = 1.0 / (window_count * lax.axis_size("dp"))
    return (
        input_total,
        summed[0] * rescale,
        summed[1] * rescale,
        summed[2] * rescale,
        summed[3] * rescale,
        summed[4] * rescale,
    )


def solution(mesh):
    in_specs = (
        P("dp", None),
        P("mp", None),
        P("mp"),
        P("mp", None),
        P("mp", None),
        P(),
        P("dp", None),
        P(),
        P("dp"),
    )
    out_specs = (
        P("dp", "mp"),
        P(("mp", "dp"), None),
        P(("mp", "dp"), None),
        P(("mp", "dp"), None),
        P(("mp", "dp")),
        P("dp"),
    )
    return jax.shard_map(
        on_device, mesh=mesh, in_specs=in_specs, out_specs=out_specs, check_vma=False
    )
```

profile of v0, /device:TPU:0, one launch (start us, length us, event | category | flops | bytes accessed | tf_op | source)
XLA Modules:
  0.0 340.6 jit_solution(8432962547412029822)
XLA Ops:
  7.2 1.7 copy-done
  8.9 2.3 convolution_add_fusion.2
  11.2 1.1 copy-done.11
  12.2 1.6 fusion.8
  13.9 3.9 %convolution_add_fusion = f32[1024,1280]{1,0:T(8,128)} fusion(f32[1024,1280]{1,0:T(8,128)S(1)} %fusion.8, bf16[320,1280]{1,0:T(8,128)(2,1)S(1)} %copy-done.5, bf16[1024,1280]{1,0:T(8,128)(2,1)S(1)} %copy-done, s32[]{:T(128)S(6)} %select_n.14), kind=kOutput, calls=%fused_computation.1 | convolution fusion | flops 840171520 | bytes 12091396 | tf_op jit(solution)/shard_map/dot_general | solution.py:86
  17.9 0.6 copy-done.7
  18.7 0.1 reshape.84
  18.8 1.6 constant_dynamic-slice_fusion
  20.4 1.6 copy.22
  22.1 2.4 broadcast_in_dim.14
  24.4 2.5 reshape.83
  26.9 2.8 copy.23
  29.7 49.0 %reduce-scatter.3.cloned.1.call-done = f32[256,1280]{1,0:T(8,128)} async-done(((f32[1024,1280]{1,0:T(8,128)}), f32[256,1280]{1,0:T(8,128)}) %reduce-scatter.3.cloned.1.call-update) | async-done | bytes 1310736 | tf_op jit(solution)/shard_map/reduce_scatter | solution.py:91
  78.7 2.1 multiply_convert_fusion
  80.8 0.2 broadcast_in_dim.31
  81.1 35.4 %all_to_all.24 = bf16[4,256,1280]{2,1,0:T(8,128)(2,1)S(1)} all-to-all(bf16[4,256,1280]{2,1,0:T(8,128)(2,1)S(1)} %broadcast_in_dim.31), channel_id=1, replica_groups=mesh['dp'=32,'mp'=4] {'mp'}, dimensions={0} | all-to-all | bytes 5242880 | tf_op jit(solution)/shard_map/all_to_all | solution.py:20
  116.5 2.1 convert_reduce_fusion.1
  118.6 2.4 fusion.7
  120.9 2.5 fusion.2
  123.5 0.2 reduce-scatter.5.cloned.1.call-start
  123.7 3.4 %fusion.11 = f32[320,1280]{1,0:T(8,128)} fusion(bf16[1024,320]{0,1:T(8,128)(2,1)} %get-tuple-element.12, bf16[1024,1280]{1,0:T(8,128)(2,1)S(1)} %copy-done), kind=kOutput, calls=%fused_computation.34 | convolution fusion | flops 838860800 | bytes 4915200 | tf_op jit(solution)/shard_map/dot_general | solution.py:104
  127.2 0.4 convert_reduce_fusion
  127.6 0.1 reshape.87
  127.7 0.1 reshape.86
  127.8 2.9 reshape_reshape.10
  130.6 3.0 reshape_reshape.11
  133.6 2.9 reshape_reshape.9
  136.5 2.9 constant_dynamic-update-slice_fusion.2
  139.3 1.3 constant_dynamic-update-slice_fusion.1
  140.6 0.7 copy-done.3
  141.3 1.3 constant_dynamic-update-slice_fusion
  142.7 1.3 dynamic-update-slice.3
  144.0 1.4 dynamic-update-slice.4
  145.4 5.0 %pad.4 = f32[32,38912]{1,0:T(8,128)} pad(f32[32,38450]{1,0:T(8,128)} %dynamic-update-slice.4, f32[]{:T(128)} %constant.4.clone.1), padding=0_0x0_462 | pad | bytes 9902340 | tf_op jit(solution)/shard_map/jit(_pad)/pad | solution.py:37
  150.4 5.4 %reshape.88 = f32[9728,128]{1,0:T(8,128)} reshape(f32[32,38912]{1,0:T(8,128)} %pad.4) | data formatting | bytes 9961472 | tf_op jit(solution)/shard_map/reshape | solution.py:37
  155.9 2.2 copy.24
  158.1 23.7 %all_to_all.25 = bf16[320,4,320]{0,2,1:T(8,128)(2,1)S(1)} all-to-all(bf16[320,4,320]{0,2,1:T(8,128)(2,1)} %bitcast.26), channel_id=1, replica_groups=mesh['dp'=32,'mp'=4] {'mp'}, dimensions={1} | all-to-all | bytes 1638400 | tf_op jit(solution)/shard_map/all_to_all | solution.py:98
  181.8 1.7 copy.25
  183.5 2.8 all_to_all.21
  186.3 3.9 %fusion.10 = f32[1024,320]{0,1:T(8,128)} fusion(bf16[1024,1280]{1,0:T(8,128)(2,1)} %bitcast.25, bf16[320,1280]{1,0:T(8,128)(2,1)S(1)} %copy-done.5), kind=kOutput, calls=%fused_computation.33 | convolution fusion | flops 838860800 | bytes 4751360 | tf_op jit(solution)/shard_map/dot_general | solution.py:97
  190.1 4.4 %convolution_add_fusion.1 = f32[1024,320]{0,1:T(8,128)} fusion(f32[1024,320]{0,1:T(8,128)} %fusion.10, bf16[1280,320]{0,1:T(8,128)(2,1)} %all_to_all.21, bf16[1024,1280]{0,1:T(8,128)(2,1)} %all-gather.2.cloned.1.call-done), kind=kOutput, calls=%fused_computation.4 | convolution fusion | flops 839188480 | bytes 6062080 | tf_op jit(solution)/shard_map/dot_general | solution.py:99
  194.6 134.2 %reduce-scatter.5.cloned.1.call-done = f32[304,128]{1,0:T(8,128)} async-done(((f32[9728,128]{1,0:T(8,128)}), f32[304,128]{1,0:T(8,128)}) %reduce-scatter.5.cloned.1.call-update) | async-done | bytes 155664 | tf_op jit(solution)/shard_map/reduce_scatter | solution.py:38
  328.8 1.3 slice_multiply_fusion.3
  330.1 1.2 slice_multiply_fusion.4
  331.2 0.9 slice_multiply_fusion
  332.2 0.6 mul.74
  332.8 0.6 mul.72
  333.4 0.6 mul.70
  (34 shorter events, 0.4 us)
Async XLA Ops:
  7.2 1.7 copy-start
  7.2 71.5 %reduce-scatter.3.cloned.1.call-start = ((), (), s32[]{:S(2)}) async-start(), calls=%async_computation.4 | async-start | bytes 6553600 | tf_op jit(solution)/shard_map/reduce_scatter | solution.py:91
  8.9 3.3 copy-start.8
  11.2 1.1 copy-start.11
  12.2 1.6 copy-start.5
  17.8 0.7 copy-start.7
  17.8 0.9 copy-start.10
  17.8 172.3 %all-gather.2.cloned.1.call-start = ((), (), s32[]{:S(2)}) async-start(), calls=%async_computation.5 | async-start | bytes 3276800 | tf_op jit(solution)/shard_map/all_gather | solution.py:100
  26.9 51.8 %copy-start.6 = (f32[1280]{0:T(1024)S(1)}, f32[1280]{0:T(1024)}, u32[]{:S(2)}) copy-start(f32[1280]{0:T(1024)} %param.14) | copy-start | bytes 15364
  81.0 35.4 %copy-start.9 = (bf16[320,1280]{1,0:T(8,128)(2,1)S(1)}, bf16[320,1280]{1,0:T(8,128)(2,1)}, u32[]{:S(2)}) copy-start(bf16[320,1280]{1,0:T(8,128)(2,1)} %param.12) | copy-start | bytes 2457604
  81.0 35.4 %copy-start.12 = (f32[1024,320]{0,1:T(8,128)S(1)}, f32[1024,320]{0,1:T(8,128)}, u32[]{:S(2)}) copy-start(f32[1024,320]{0,1:T(8,128)} %copy-done.11) | copy-start | bytes 3932164
  116.5 4.5 %copy-start.1 = (bf16[4,256,1280]{2,1,0:T(8,128)(2,1)}, bf16[4,256,1280]{2,1,0:T(8,128)(2,1)S(1)}, u32[]{:S(2)}) copy-start(bf16[4,256,1280]{2,1,0:T(8,128)(2,1)S(1)} %all_to_all.24) | copy-start | bytes 7864324
  123.5 205.3 %reduce-scatter.5.cloned.1.call-start = ((), (), s32[]{:S(2)}) async-start(), calls=%async_computation.6 | async-start | bytes 5136384 | tf_op jit(solution)/shard_map/reduce_scatter | solution.py:38
  123.7 3.4 %copy-start.2 = (bf16[4,256,1280]{2,1,0:T(8,128)(2,1)S(1)}, bf16[4,256,1280]{2,1,0:T(8,128)(2,1)}, u32[]{:S(2)}) copy-start(bf16[4,256,1280]{2,1,0:T(8,128)(2,1)} %copy-done.1) | copy-start | bytes 7864324
  136.5 2.9 copy-start.4
  139.3 2.0 copy-start.3
Sparse Core Ops, SparseCore 0:
  17.9 60.7 reduce-scatter.2
  123.6 28.4 all-gather.1
  156.0 172.7 reduce-scatter.4
where the time goes:
time: 342 us; the launch traced here: 341 us
  waiting for transfers between devices  183 us (54%)
  blocking collectives  59.1 us (17%)
  local copies, waits for them, and re-layouts  51.5 us (15%)
  matrix products  26.5 us (8%)
  between operations  13.9 us (4%)
  other arithmetic  6.05 us (2%)
    reduce_scatter x1, waiting for transfers between devices, sum_packed(): lax.psum_scatter(lines, axis, tiled=True).reshape(-1)  134 us
    reduce_scatter x1, waiting for transfers between devices, on_device(): lax.psum_scatter(partial_out, 'mp', scatter_dimension=0, tiled=True)  49 us
    all_to_all x1, blocking collectives, copy_for_each(): return lax.all_to_all(copies, axis, split_axis=0, concat_axis=0, tiled=True)  35.4 us
    all_to_all x1, blocking collectives, on_device(): lax.all_to_all(inner_weight, 'mp', split_axis=1, concat_axis=0, tiled=True)  23.7 us
    unnamed x31, local copies, waits for them, and re-layouts  13.1 us
    another operation x3, local copies, waits for them, and re-layouts, sum_packed(): lines = jnp.concatenate([b.reshape(length, -1) for b in tiles], axis=1)  8.68 us
  transfers between devices with their start and end apart: 3, of which 2 were waited for; matrix products, arithmetic and copies ran while one was open for 16% of the time, Pallas kernels for 0%

commit v1 on v0

v1 whole, which is shorter than its diff:
```python
import jax
import jax.numpy as jnp
from jax import lax
from jax.experimental import pallas as pl
from jax.experimental.pallas import tpu as pltpu
from jax.sharding import PartitionSpec as P

MESH = pl.DeviceIdType.MESH
F32 = jnp.float32
BF16 = jnp.bfloat16
LEVELS = 9
PATCHES = 16
QUANTILES = 10
HUBER_WIDTH = 0.5

D = 1280
SHARD = 320
PAD = 384
HALF = 2 * PAD
CHIP = 512
CORE = 256
OWN = 640
C1, C2, C3 = 160, 40, 10
LANES = 640

NN = (((1,), (0,)), ((), ()))
NT = (((1,), (1,)), ((), ()))


def mm(a, b, dims=NN):
    return lax.dot_general(a, b, dims, preferred_element_type=F32)


def rem(a, n):
    return lax.rem(a, jnp.int32(n))


def div(a, n):
    return lax.div(a, jnp.int32(n))


def part(index, size):
    return pl.ds(pl.multiple_of(index * size, size), size)


ORDERS = ("xyz", "yzx", "zxy")


def split(n, size):
    q = (
        (n >= size).astype(jnp.int32)
        + (n >= 2 * size).astype(jnp.int32)
        + (n >= 3 * size).astype(jnp.int32)
    )
    return q, n - q * size


def natural(n, order):
    d1, n = split(n, C1)
    d2, n = split(n, C2)
    d3, r = split(n, C3)
    at = dict(zip(order, (d1, d2, d3)))
    x_hi = (at["x"] >= 2).astype(jnp.int32)
    x_lo = at["x"] - 2 * x_hi
    return x_hi * PAD + (at["z"] * 8 + x_lo * 4 + at["y"]) * 10 + r


def kernel(
    series_hbm, wi_hbm, wo_hbm, ws_hbm, ib_hbm, ob_hbm, targets_hbm, levels_ref, counts_ref,
    in_out, gi_out, go_out, gs_out, ib_out, ob_out,
    S, Wi, Wo, Ws, IB, OB, T, sel, perm, isel, isel_send, sH, H, DV, LT, HG, OG,
    spread, tau, p_send, p_recv, p_own, G, ST, RA, RD, RSUM, T2, acc1, ST2, R2, acc2, F3, ST3, R3,
    bsend, brecv, igf, ig_send, ig_recv, outs,
    lsem, ssem, rsem,
):
    dp = lax.axis_index("dp")
    mp = lax.axis_index("mp")
    core = rem(mp, 2)
    x_hi = div(mp, 2)
    z = div(dp, 8)
    x_lo = rem(div(dp, 4), 2)
    y = rem(dp, 4)
    x = x_hi * 2 + x_lo
    other_hi = 1 - x_hi

    def device(x, y, z, core):
        return {"dp": z * 8 + rem(x, 2) * 4 + y, "mp": div(x, 2) * 2 + core}

    pos = {"x": x, "y": y, "z": z}

    def along(axis, k):
        at = dict(pos)
        at[axis] = rem(at[axis] + k, 4)
        return device(at["x"], at["y"], at["z"], core)

    partner = device(x, y, z, 1 - core)
    cross = device(3 - x, y, z, core)
    beside = device(x + 1 - 2 * x_lo, y, z, core)

    loads = []

    def load(src, dst):
        c = pltpu.make_async_copy(src, dst, lsem.at[len(loads)])
        c.start()
        loads.append(c)
        return c

    own_rows = pl.ds(pl.multiple_of(x_hi * PAD, 128), SHARD)
    l_i = load(wi_hbm, Wi.at[own_rows, :])
    l_s = load(ws_hbm, Ws.at[own_rows, :])
    l_o = load(wo_hbm, Wo.at[own_rows, :])
    l_ib = load(ib_hbm, IB.at[x_hi])
    l_series = load(series_hbm.at[part(x_hi, CHIP), :], S)
    l_t = load(targets_hbm.at[part(x_hi * 2 + core, CORE), :], T)
    l_ob = load(ob_hbm, OB)

    barrier = pltpu.get_barrier_semaphore()
    peers = [partner] + [along(a, k) for a in "xyz" for k in (1, 2, 3)]
    for peer in peers:
        pl.semaphore_signal(barrier, inc=1, device_id=peer, device_id_type=MESH)
    pl.semaphore_wait(barrier, len(peers))

    sent = []

    def send(src, dst, to):
        i = len(sent)
        c = pltpu.make_async_remote_copy(
            src_ref=src, dst_ref=dst, send_sem=ssem.at[i], recv_sem=rsem.at[i],
            device_id=to, device_id_type=MESH,
        )
        c.start()
        sent.append(c)
        return c

    weights = (Wi, Ws, Wo)
    axis_of = (y, z)

    def quarter(w, hi, color, q, lanes=None):
        start, size = lanes or (0, LANES)
        return weights[w].at[
            pl.ds(pl.multiple_of(hi * PAD + q * 80, 16), 80),
            pl.ds(pl.multiple_of(color * LANES + start, 128), size),
        ]

    def on_color(color, a, b):
        return jnp.where(color == 0, a, b)

    first, second = x_lo, 1 - x_lo

    def ring(color):
        up = {k: on_color(color, along("y", 1)[k], along("z", 1)[k]) for k in ("dp", "mp")}
        down = {k: on_color(color, along("y", 3)[k], along("z", 3)[k]) for k in ("dp", "mp")}
        return on_color(color, y, z), up, down

    for l in (l_i, l_s, l_o, l_ib):
        l.wait()
    crossed = []
    for w in range(3):
        q = on_color(second, y, z)
        piece = quarter(w, x_hi, second, q)
        crossed.append(send(piece, piece, cross))
    b_crossed = send(IB.at[x_hi], IB.at[x_hi], cross)

    for W in weights:
        for j in range(2):
            W[pl.ds(j * PAD + SHARD, PAD - SHARD), :] = jnp.zeros((PAD - SHARD, D), BF16)

    def one_hot_sel(k):
        def body(i, _):
            h = lax.broadcasted_iota(jnp.int32, (128, D), 0) + i * 128
            col = lax.broadcasted_iota(jnp.int32, (128, D), 1)
            hi = (h >= PAD).astype(jnp.int32)
            j = h - hi * PAD
            want = hi * 640 + k * SHARD + j
            sel[part(i, 128), :] = jnp.where((col == want) & (j < SHARD), 1.0, 0.0).astype(BF16)
            return 0

        lax.fori_loop(0, HALF // 128, body, 0)

    def first_forward(w):
        q, up, down = ring(first)
        crossed[w].wait_recv()
        piece = quarter(w, other_hi, first, q)
        return send(piece, piece, beside), send(piece, piece, up), send(piece, piece, down)

    def second_forward(w, c):
        q, up, down = ring(second)
        c.wait_recv()
        piece = quarter(w, other_hi, second, q)
        return send(piece, piece, up), send(piece, piece, down)

    def relay(w, color, from_below, from_above):
        q, up, down = ring(color)
        cut = PAD if w % 2 == 0 else 256
        from_below.wait_recv()
        a = quarter(w, other_hi, color, rem(q + 3, 4), (0, cut))
        s1 = send(a, a, up)
        from_above.wait_recv()
        b = quarter(w, other_hi, color, rem(q + 1, 4), (cut, LANES - cut))
        return s1, send(b, b, down)

    one_hot_sel(core)
    l_series.wait()

    def sel_body(i, _):
        sH[:, part(i, 256)] = mm(S[...], sel[part(i, 256), :], NT).astype(BF16)
        return 0

    f0 = first_forward(0)
    lax.fori_loop(0, 3, sel_body, 0)
    f1 = first_forward(1)

    for k in range(3):
        def perm_body(i, _, k=k):
            n = lax.broadcasted_iota(jnp.int32, (128, 128), 0) + i * 128
            want = natural(n, ORDERS[k])
            lane = lax.broadcasted_iota(jnp.int32, (128, 128), 1)
            for t in range(HALF // 128):
                perm[k, part(i, 128), pl.ds(t * 128, 128)] = jnp.where(
                    lane + t * 128 == want, 1.0, 0.0
                ).astype(BF16)
            return 0

        lax.fori_loop(0, OWN // 128, perm_body, 0)
        if k == 0:
            s0 = second_forward(0, f0[0])
            r0 = relay(0, first, f0[1], f0[2])
            f2 = first_forward(2)

    def transposed(k, src):
        def body(i, _):
            LT[k, :, part(i, 256)] = mm(perm[k], src[part(i, 256), :], NT).astype(BF16)
            return 0

        lax.fori_loop(0, CHIP // 256, body, 0)

    s1 = second_forward(1, f1[0])
    r1 = relay(1, first, f1[1], f1[2])
    transposed(0, sH)
    s2 = second_forward(2, f2[0])
    r0b = relay(0, second, s0[0], s0[1])

    l_t.wait()
    l_ob.wait()
    col = lax.broadcasted_iota(jnp.int32, (128, D), 1)
    row = lax.broadcasted_iota(jnp.int32, (128, D), 0)
    off = col - row * QUANTILES
    spreader = jnp.where((off >= 0) & (off < QUANTILES), 1.0, 0.0).astype(F32)
    spread[...] = (
        lax.dot_general(
            T[...], spreader, NN, precision=lax.Precision.HIGHEST, preferred_element_type=F32
        )
        - OB[...]
    )
    levels_rows = jnp.zeros((128, D), F32)
    for c in range(QUANTILES):
        level = (jnp.full((128, D), levels_ref[c], jnp.int32).astype(F32) + 1.0) / (LEVELS + 1)
        levels_rows = levels_rows + jnp.where(off == c, level, 0.0)
    tau[...] = jnp.sum(levels_rows, axis=0, keepdims=True)

    r2 = relay(2, first, f2[1], f2[2])
    r1b = relay(1, second, s1[0], s1[1])
    for c in r0 + r0b:
        c.wait_recv()
    b_crossed.wait_recv()

    def hidden_body(i, _):
        cols = part(i, 128)
        bias = IB[div(i, 3), :, part(rem(i, 3), 128)]
        pre = mm(S[...], Wi[part(i, 128), :], NT) + bias
        sig = jax.nn.sigmoid(pre)
        H[:, cols] = (pre * sig).astype(BF16)
        DV[:, cols] = sig * (1.0 + pre * (1.0 - sig))
        return 0

    lax.fori_loop(0, HALF // 128, hidden_body, 0)
    r2b = relay(2, second, s2[0], s2[1])
    transposed(1, H)
    for c in r1 + r1b + r2 + r2b:
        c.wait_recv()

    def predict(rows, dst):
        def body(i, _):
            cols = part(i, 256)
            dst[:, cols] = mm(H[rows, :], Wo[:, cols]) + mm(sH[rows, :], Ws[:, cols])
            return 0

        lax.fori_loop(0, D // 256, body, 0)

    mine, theirs = part(core, CORE), part(1 - core, CORE)
    predict(theirs, p_send)
    p_copy = send(p_send, p_recv, partner)
    predict(mine, p_own)
    p_copy.wait_recv()

    def slope_body(w, _):
        rows = part(w, PATCHES)
        count = counts_ref[(x_hi * 2 + core) * (CORE // PATCHES) + w]
        counted = jnp.full((PATCHES, 128), count, jnp.int32)
        valid = lax.broadcasted_iota(jnp.int32, (PATCHES, 128), 0) < counted
        weight = (jnp.where(valid, 1.0, 0.0) / counted.astype(F32))[:, :1]
        residue = spread[rows, :] - (p_own[rows, :] + p_recv[rows, :])
        t = tau[...]
        slopes = jnp.where(residue >= 0, t, 1.0 - t) * jnp.clip(residue / HUBER_WIDTH, -1.0, 1.0)
        OG[pl.ds(pl.multiple_of(core * CORE + w * PATCHES, PATCHES), PATCHES), :] = (
            -slopes * weight
        ).astype(BF16)
        return 0

    lax.fori_loop(0, CORE // PATCHES, slope_body, 0)
    og_copy = send(OG.at[mine, :], OG.at[mine, :], partner)

    def isel_body(dst):
        def body(i, _):
            dst[:, part(i, 256)] = mm(Wi[...], sel[part(i, 256), :], NT).astype(BF16)
            return 0

        lax.fori_loop(0, HALF // 256, body, 0)

    og_copy.wait_recv()

    def halves(h):
        return pl.ds(h * LANES, LANES)

    def chunk(p, k):
        return part(rem(p + k, 4), C1)

    def gradient(k, right):
        def body(i, _):
            cols = part(i, 256)
            g = mm(LT[k], right[:, cols])
            G[k, :, cols] = g
            ST[k, :, cols] = g.astype(BF16)
            return 0

        lax.fori_loop(0, D // 256, body, 0)
        axis = ORDERS[k][0]
        p = pos[axis]
        up, down = along(axis, 1), along(axis, 3)
        return (
            send(ST.at[k, chunk(p, 2), halves(0)], RA.at[k, 0], up),
            send(ST.at[k, chunk(p, 2), halves(1)], RA.at[k, 1], down),
            send(ST.at[k, chunk(p, 1), halves(1)], RD.at[k, 0], up),
            send(ST.at[k, chunk(p, 3), halves(0)], RD.at[k, 1], down),
        )

    def pass_on(k, step):
        axis = ORDERS[k][0]
        p = pos[axis]
        out = []
        for h, hop in ((0, 1), (1, 3)):
            step[h].wait_recv()

            def body(i, _, h=h, hop=hop):
                rows = pl.ds(pl.multiple_of(rem(p + hop, 4) * C1 + i * 32, 32), 32)
                T2[k, h, part(i, 32), :] = (
                    G[k, rows, halves(h)] + RA[k, h, part(i, 32), :].astype(F32)
                ).astype(BF16)
                return 0

            lax.fori_loop(0, C1 // 32, body, 0)
            out.append(send(T2.at[k, h], RSUM.at[k, h], along(axis, hop)))
        return out

    def second_phase(k, step, passed):
        p = pos[ORDERS[k][0]]
        for c in (step[2], step[3], passed[0], passed[1]):
            c.wait_recv()

        def body(i, _):
            here = part(i, 32)
            rows = pl.ds(pl.multiple_of(p * C1 + i * 32, 32), 32)
            for h in range(2):
                acc1[k, here, halves(h)] = (
                    G[k, rows, halves(h)]
                    + RSUM[k, h, here, :].astype(F32)
                    + RD[k, 1 - h, here, :].astype(F32)
                )
            return 0

        lax.fori_loop(0, C1 // 32, body, 0)
        for q in range(4):
            ST2[k, q] = acc1[k, pl.ds(q * C2, C2), :].astype(BF16)
        axis = ORDERS[k][1]
        p2 = pos[axis]
        return [send(ST2.at[k, rem(p2 + o, 4)], R2.at[k, o - 1], along(axis, o)) for o in (1, 3, 2)]

    def third_phase(k, step):
        axis = ORDERS[k][1]
        p2 = pos[axis]
        for c in step:
            c.wait_recv()
        total = acc1[k, pl.ds(pl.multiple_of(p2 * C2, 8), C2), :]
        for o in range(3):
            total = total + R2[k, o].astype(F32)
        acc2[k] = total
        for q in range(4):
            piece = acc2[k, pl.ds(q * C3, C3), :]
            F3[k, q] = piece
            ST3[k, q] = piece.astype(BF16)
        axis = ORDERS[k][2]
        p3 = pos[axis]
        return [send(ST3.at[k, rem(p3 + o, 4)], R3.at[k, o - 1], along(axis, o)) for o in (1, 3, 2)]

    rescale = 1.0 / 2048

    def finish(k, step, out):
        p3 = pos[ORDERS[k][2]]
        for c in step:
            c.wait_recv()
        total = F3[k, p3]
        for o in range(3):
            total = total + R3[k, o].astype(F32)
        out[...] = total * rescale

    skip1 = gradient(0, OG)
    outer1 = gradient(1, OG)

    def backflow_body(i, _):
        cols = part(i, 256)
        back = mm(OG[...], Wo[cols, :], NT)
        HG[core, :, cols] = (back * DV[:, cols]).astype(BF16)
        return 0

    lax.fori_loop(0, HALF // 256, backflow_body, 0)
    hg_copy = send(HG.at[core], HG.at[core], partner)
    transposed(2, HG.at[core])
    inner1 = gradient(2, S)

    bsend[0, :, pl.ds(0, HALF)] = jnp.sum(HG[core].astype(F32), axis=0, keepdims=True)
    bsend[0, :, pl.ds(HALF, D)] = jnp.sum(OG[...].astype(F32), axis=0, keepdims=True)

    def bias_send(i):
        axis = "xyz"[i]
        return [send(bsend.at[i], brecv.at[i, o - 1], along(axis, o)) for o in (1, 2, 3)]

    def bias_add(i, copies):
        for c in copies:
            c.wait_recv()
        bsend[i + 1] = bsend[i] + brecv[i, 0] + brecv[i, 1] + brecv[i, 2]

    bias1 = bias_send(0)
    isel_body(isel.at[core])
    skip2 = pass_on(0, skip1)
    one_hot_sel(1 - core)
    isel_body(isel_send)
    isel_copy = send(isel_send, isel.at[core], partner)
    outer2 = pass_on(1, outer1)
    bias_add(0, bias1)
    bias2 = bias_send(1)
    inner2 = pass_on(2, inner1)

    hg_copy.wait_recv()
    isel_copy.wait_recv()

    def input_body(i, _):
        cols = part(i, 256)
        igf[:, cols] = (
            mm(HG[0], isel[0, :, cols])
            + mm(HG[1], isel[1, :, cols])
            + mm(OG[...], Ws[cols, :], NT)
        )
        return 0

    lax.fori_loop(0, HALF // 256, input_body, 0)
    ig_send[...] = igf[:, part(other_hi, PAD)].astype(BF16)
    ig_copy = send(ig_send, ig_recv, along("x", 2))
    outs[0] = igf[:, part(x_hi, PAD)][:, :SHARD]
    out0 = pltpu.make_async_copy(outs.at[0], in_out.at[part(x_hi, CHIP), :], lsem.at[len(loads)])
    out0.start()

    skip3 = second_phase(0, skip1, skip2)
    outer3 = second_phase(1, outer1, outer2)
    bias_add(1, bias2)
    bias3 = bias_send(2)
    inner3 = second_phase(2, inner1, inner2)
    skip4 = third_phase(0, skip3)
    outer4 = third_phase(1, outer3)
    ig_copy.wait_recv()
    outs[1] = ig_recv[:, :SHARD].astype(F32)
    out1 = pltpu.make_async_copy(
        outs.at[1], in_out.at[part(other_hi, CHIP), :], lsem.at[len(loads) + 1]
    )
    out1.start()
    inner4 = third_phase(2, inner3)
    bias_add(2, bias3)

    def pick(v, start):
        n = v.shape[1]
        i = lax.broadcasted_iota(jnp.int32, (n, 128), 0)
        j = lax.broadcasted_iota(jnp.int32, (n, 128), 1)
        hot = jnp.where(i == j + start, 1.0, 0.0).astype(F32)
        return lax.dot_general(
            jnp.broadcast_to(v, (8, n)), hot, NN,
            precision=lax.Precision.HIGHEST, preferred_element_type=F32,
        )[:1] * rescale

    ib_out[...] = pick(bsend[3, :, pl.ds(0, HALF)], x_hi * PAD + dp * 10)[:, :10]
    ob_out[...] = pick(bsend[3, :, pl.ds(HALF, D)], dp * 40)[:, :40]
    finish(0, skip4, gs_out)
    finish(1, outer4, go_out)
    finish(2, inner4, gi_out)
    for c in sent:
        c.wait_send()
    out0.wait()
    out1.wait()


N_SENDS = 96


def on_device(series, wi, ib, wo, ws, ob, targets, levels, counts):
    hbm = pl.BlockSpec(memory_space=pl.ANY)
    vmem = pl.BlockSpec(memory_space=pltpu.VMEM)
    smem = pl.BlockSpec(memory_space=pltpu.SMEM)
    grad = jax.ShapeDtypeStruct((C3, D), F32)
    outs = pl.pallas_call(
        kernel,
        out_shape=(
            jax.ShapeDtypeStruct((2 * CHIP, SHARD), F32), grad, grad, grad,
            jax.ShapeDtypeStruct((1, 10), F32), jax.ShapeDtypeStruct((1, 40), F32),
        ),
        in_specs=[hbm] * 7 + [smem] * 2,
        out_specs=(hbm,) + (vmem,) * 5,
        scratch_shapes=[
            pltpu.VMEM((CHIP, D), BF16),
            pltpu.VMEM((HALF, D), BF16),
            pltpu.VMEM((HALF, D), BF16),
            pltpu.VMEM((HALF, D), BF16),
            pltpu.VMEM((2, 1, PAD), F32),
            pltpu.VMEM((1, D), F32),
            pltpu.VMEM((CORE, 128), F32),
            pltpu.VMEM((HALF, D), BF16),
            pltpu.VMEM((3, OWN, HALF), BF16),
            pltpu.VMEM((2, HALF, HALF), BF16),
            pltpu.VMEM((HALF, HALF), BF16),
            pltpu.VMEM((CHIP, HALF), BF16),
            pltpu.VMEM((CHIP, HALF), BF16),
            pltpu.VMEM((CHIP, HALF), F32),
            pltpu.VMEM((3, OWN, CHIP), BF16),
            pltpu.VMEM((2, CHIP, HALF), BF16),
            pltpu.VMEM((CHIP, D), BF16),
            pltpu.VMEM((CORE, D), F32),
            pltpu.VMEM((1, D), F32),
            pltpu.VMEM((CORE, D), F32),
            pltpu.VMEM((CORE, D), F32),
            pltpu.VMEM((CORE, D), F32),
            pltpu.VMEM((3, OWN, D), F32),
            pltpu.VMEM((3, OWN, D), BF16),
            pltpu.VMEM((3, 2, C1, LANES), BF16),
            pltpu.VMEM((3, 2, C1, LANES), BF16),
            pltpu.VMEM((3, 2, C1, LANES), BF16),
            pltpu.VMEM((3, 2, C1, LANES), BF16),
            pltpu.VMEM((3, C1, D), F32),
            pltpu.VMEM((3, 4, C2, D), BF16),
            pltpu.VMEM((3, 3, C2, D), BF16),
            pltpu.VMEM((3, C2, D), F32),
            pltpu.VMEM((3, 4, C3, D), F32),
            pltpu.VMEM((3, 4, C3, D), BF16),
            pltpu.VMEM((3, 3, C3, D), BF16),
            pltpu.VMEM((4, 1, HALF + D), F32),
            pltpu.VMEM((3, 3, 1, HALF + D), F32),
            pltpu.VMEM((CHIP, HALF), F32),
            pltpu.VMEM((CHIP, PAD), BF16),
            pltpu.VMEM((CHIP, PAD), BF16),
            pltpu.VMEM((2, CHIP, SHARD), F32),
            pltpu.SemaphoreType.DMA((16,)),
            pltpu.SemaphoreType.DMA((N_SENDS,)),
            pltpu.SemaphoreType.DMA((N_SENDS,)),
        ],
        compiler_params=pltpu.CompilerParams(
            collective_id=0, has_side_effects=True, vmem_limit_bytes=62 * 1024 * 1024
        ),
    )(
        series, wi, wo, ws, jnp.pad(ib, (0, PAD - SHARD)).reshape(1, PAD), ob.reshape(1, D),
        targets, levels, counts,
    )
    input_grad, inner, outer, skip, inbias, outbias = outs
    return input_grad, inner, outer, skip, inbias.reshape(10), outbias.reshape(40)


def solution(mesh):
    return jax.shard_map(
        on_device,
        mesh=mesh,
        in_specs=(
            P("dp", None), P("mp", None), P("mp"), P("mp", None), P("mp", None), P(None),
            P("dp", None), P(None), P("dp"),
        ),
        out_specs=(
            P("dp", "mp"), P(("mp", "dp"), None), P(("mp", "dp"), None), P(("mp", "dp"), None),
            P(("mp", "dp")), P("dp"),
        ),
        check_vma=False,
    )
```

time: 342 us -> 92.6 us (0.27)
  waiting for transfers between devices: 183 us -> 0 us
  Pallas kernels: 0 us -> 82.3 us
  blocking collectives: 59.1 us -> 0 us
  local copies, waits for them, and re-layouts: 51.5 us -> 8.49 us
  matrix products: 26.5 us -> 0 us
  between operations: 13.9 us -> 0.69 us
  other arithmetic: 6.05 us -> 0 us
    reduce_scatter x2 -> x0, waiting for transfers between devices: 183 us -> none  [the longest x1 134 us: sum_packed(): lax.psum_scatter(lines, axis, tiled=True).reshape(-1)]
    pallas_call x0 -> x1, Pallas kernels: none -> 82.3 us  [on_device(): pl.pallas_call(kernel, out_shape=(jax.ShapeDtypeStruct((2 * CHIP, SHARD),...]
    all_to_all x2 -> x0, blocking collectives: 59.1 us -> none  [the longest x1 35.4 us: copy_for_each(): return lax.all_to_all(copies, axis, split_axis=0, concat_axis=0, tiled=True)]
    dot_general x9 -> x0, matrix products: 26.5 us -> none  [the longest x1 4.42 us: on_device(): jnp.dot(lax.all_gather(hidden_grad, 'mp', axis=1, tiled=True), columns, p...]
    reshape x6 -> x2, local copies, waits for them, and re-layouts: 11 us -> 1.86 us  [the longest x1 1.29 us: on_device(): ob.reshape(1, D)]
    another operation x3 -> x0, local copies, waits for them, and re-layouts: 8.68 us -> none  [sum_packed(): lines = jnp.concatenate([b.reshape(length, -1) for b in tiles], axis=1)]
    unnamed x31 -> x16, local copies, waits for them, and re-layouts: 13.1 us -> 5.94 us
    all_to_all x2 -> x0, local copies, waits for them, and re-layouts: 4.46 us -> none  [on_device(): lax.all_to_all(inner_weight, 'mp', split_axis=1, concat_axis=0, tiled=True)]
  transfers between devices with their start and end apart: 3 -> 0, of which waited for: 2 -> 0; matrix products, arithmetic and copies ran while one was open for 16% -> 0% of each run, Pallas kernels for 0% -> 0%
where the time goes in v1:
time: 92.6 us; the launch traced here: 91.5 us
  Pallas kernels  82.3 us (89%)
  local copies, waits for them, and re-layouts  8.49 us (9%)
    pallas_call x1, Pallas kernels, on_device(): pl.pallas_call(kernel, out_shape=(jax.ShapeDtypeStruct((2 * CHIP, SHARD),...  82.3 us
    unnamed x16, local copies, waits for them, and re-layouts  5.94 us

profile of v1, /device:TPU:0, one launch (start us, length us, event | category | flops | bytes accessed | tf_op | source)
XLA Modules:
  0.0 91.5 jit_solution(13288370545080275072)
XLA Ops:
  0.6 0.7 pad.4
  1.3 0.6 reshape.24.ib_hbm
  1.9 1.3 %reshape.25.ob_hbm = f32[1,1280]{1,0:T(1,128)} reshape(f32[1280]{0:T(1024)} %param.14) | data formatting | bytes 10240 | tf_op jit(solution)/shard_map/reshape | solution.py:575
  3.2 82.3 %shard_map.136 = (f32[1024,320]{1,0:T(8,128)}, f32[10,1280]{1,0:T(8,128)}, f32[10,1280]{1,0:T(8,128)}, f32[10,1280]{1,0:T(8,128)}, f32[1,10]{1,0:T(1,128)}, /*index=5*/f32[1,40]{1,0:T(1,128)}) custom-call(bf16[1024,1280]{1,0:T(8,128)(2,1)} %series_hbm.1, bf16[320,1280]{1,0:T(8,128)(2,1)} %wi_hbm.1, bf16[320,1280]{1,0:T(8,128)(2,1)} %wo_hbm.1, ...), custom_call_target="tpu_custom_call" | custom-call | tf_op jit(solution)/shard_map/pallas_call | solution.py:517
  85.5 0.0 copy-start.2
  85.5 0.0 copy-start.1
  85.5 0.0 copy-start
  85.6 0.0 copy-start.4
  85.6 0.0 copy-start.3
  85.6 3.0 %copy.15 = f32[1024,320]{0,1:T(8,128)} copy(f32[1024,320]{1,0:T(8,128)} %get-tuple-element.18) | data formatting | bytes 2621440
  88.6 0.0 copy-done.2
  88.6 0.6 copy.21
  89.2 0.0 copy-done.1
  89.2 0.6 copy.22
  89.8 0.0 copy-done
  89.9 0.6 copy.23
  90.5 0.0 copy-done.4
  90.5 0.5 copy.24
  91.0 0.0 copy-done.3
  91.0 0.5 copy.25
Async XLA Ops:
  85.5 3.0 %copy-start.2 = (f32[10,1280]{1,0:T(8,128)S(1)}, f32[10,1280]{1,0:T(8,128)}, u32[]{:S(2)}) copy-start(f32[10,1280]{1,0:T(8,128)} %get-tuple-element.31) | copy-start | bytes 153604
  85.5 3.7 %copy-start.1 = (f32[10,1280]{1,0:T(8,128)S(1)}, f32[10,1280]{1,0:T(8,128)}, u32[]{:S(2)}) copy-start(f32[10,1280]{1,0:T(8,128)} %get-tuple-element.32) | copy-start | bytes 153604
  85.5 4.3 %copy-start = (f32[10,1280]{1,0:T(8,128)S(1)}, f32[10,1280]{1,0:T(8,128)}, u32[]{:S(2)}) copy-start(f32[10,1280]{1,0:T(8,128)} %get-tuple-element.33) | copy-start | bytes 153604
  85.6 4.9 %copy-start.4 = (f32[1,10]{1,0:T(1,128)S(1)}, f32[1,10]{1,0:T(1,128)}, u32[]{:S(2)}) copy-start(f32[1,10]{1,0:T(1,128)} %get-tuple-element.16) | copy-start | bytes 124
  85.6 5.4 %copy-start.3 = (f32[1,40]{1,0:T(1,128)S(1)}, f32[1,40]{1,0:T(1,128)}, u32[]{:S(2)}) copy-start(f32[1,40]{1,0:T(1,128)} %get-tuple-element.17) | copy-start | bytes 484

commit v2 on v1

v2 whole, which is shorter than its diff:
```python
import jax
import jax.numpy as jnp
from jax import lax
from jax.experimental import pallas as pl
from jax.experimental.pallas import tpu as pltpu
from jax.sharding import PartitionSpec as P

MESH = pl.DeviceIdType.MESH
F32 = jnp.float32
BF16 = jnp.bfloat16
LEVELS = 9
PATCHES = 16
QUANTILES = 10
HUBER_WIDTH = 0.5

D = 1280
SHARD = 320
PAD = 384
HALF = 2 * PAD
CHIP = 512
CORE = 256
OWN = 640
C1, C2, C3 = 160, 40, 10
LANES = 640

NN = (((1,), (0,)), ((), ()))
NT = (((1,), (1,)), ((), ()))


def mm(a, b, dims=NN):
    return lax.dot_general(a, b, dims, preferred_element_type=F32)


def rem(a, n):
    return lax.rem(a, jnp.int32(n))


def div(a, n):
    return lax.div(a, jnp.int32(n))


def part(index, size):
    return pl.ds(pl.multiple_of(index * size, size), size)


ORDERS = ("xyz", "yzx", "zyx")


def split(n, size):
    q = (
        (n >= size).astype(jnp.int32)
        + (n >= 2 * size).astype(jnp.int32)
        + (n >= 3 * size).astype(jnp.int32)
    )
    return q, n - q * size


def natural(n, order):
    d1, n = split(n, C1)
    d2, n = split(n, C2)
    d3, r = split(n, C3)
    at = dict(zip(order, (d1, d2, d3)))
    x_hi = (at["x"] >= 2).astype(jnp.int32)
    x_lo = at["x"] - 2 * x_hi
    return x_hi * PAD + (at["z"] * 8 + x_lo * 4 + at["y"]) * 10 + r


def kernel(
    series_hbm, wi_hbm, wo_hbm, ws_hbm, ib_ref, ob_ref, targets_hbm, levels_ref, counts_ref,
    in_out, gi_out, go_out, gs_out, ib_out, ob_out,
    S, Wi, Wo, Ws, IB, T, sel, perm, isel, isel_send, sH, H, DV, LT, HG, OG,
    spread, tau, p_send, p_recv, p_own, G, ST, RA, RD, RSUM, T2,
    acc1, ST2, RA2, RD2, RSUM2, T3, acc2, F3, ST3, R3,
    bsend, brecv, igf, ig_send, ig_mid, ig_recv, outs,
    lsem, ssem, rsem,
):
    dp = lax.axis_index("dp")
    mp = lax.axis_index("mp")
    core = rem(mp, 2)
    x_hi = div(mp, 2)
    z = div(dp, 8)
    x_lo = rem(div(dp, 4), 2)
    y = rem(dp, 4)
    x = x_hi * 2 + x_lo
    other_hi = 1 - x_hi

    def device(x, y, z, core):
        return {"dp": z * 8 + rem(x, 2) * 4 + y, "mp": div(x, 2) * 2 + core}

    pos = {"x": x, "y": y, "z": z}

    def along(axis, k):
        at = dict(pos)
        at[axis] = rem(at[axis] + k, 4)
        return device(at["x"], at["y"], at["z"], core)

    partner = device(x, y, z, 1 - core)
    cross = device(3 - x, y, z, core)
    beside = device(x + 1 - 2 * x_lo, y, z, core)

    loads = []

    def load(src, dst):
        c = pltpu.make_async_copy(src, dst, lsem.at[len(loads)])
        c.start()
        loads.append(c)
        return c

    own_rows = pl.ds(pl.multiple_of(x_hi * PAD, 128), SHARD)
    l_i = load(wi_hbm, Wi.at[own_rows, :])
    l_s = load(ws_hbm, Ws.at[own_rows, :])
    l_o = load(wo_hbm, Wo.at[own_rows, :])
    l_series = load(series_hbm.at[part(x_hi, CHIP), :], S)
    l_t = load(targets_hbm.at[part(x_hi * 2 + core, CORE), :], T)

    IB[:, part(x_hi, PAD)] = jnp.concatenate(
        [ib_ref[...].reshape(1, SHARD), jnp.zeros((1, PAD - SHARD), F32)], axis=1
    )
    barrier = pltpu.get_barrier_semaphore()
    peers = [partner] + [along(a, k) for a in "xyz" for k in (1, 2, 3)]
    for peer in peers:
        pl.semaphore_signal(barrier, inc=1, device_id=peer, device_id_type=MESH)
    pl.semaphore_wait(barrier, len(peers))

    sent = []

    def send(src, dst, to):
        i = len(sent)
        c = pltpu.make_async_remote_copy(
            src_ref=src, dst_ref=dst, send_sem=ssem.at[i], recv_sem=rsem.at[i],
            device_id=to, device_id_type=MESH,
        )
        c.start()
        sent.append(c)
        return c

    weights = (Wi, Ws, Wo)
    axis_of = (y, z)

    def quarter(w, hi, color, q, start, size):
        return weights[w].at[
            pl.ds(pl.multiple_of(hi * PAD + q * 80, 16), 80),
            pl.ds(pl.multiple_of(color * LANES + start, 128), size),
        ]

    def on_color(color, a, b):
        return jnp.where(color == 0, a, b)

    first, second = x_lo, 1 - x_lo

    def ring(color):
        up = {k: on_color(color, along("y", 1)[k], along("z", 1)[k]) for k in ("dp", "mp")}
        down = {k: on_color(color, along("y", 3)[k], along("z", 3)[k]) for k in ("dp", "mp")}
        return on_color(color, y, z), up, down

    items = [
        (w, start, size, cut)
        for w in range(3)
        for start, size, cut in ((0, 384, 256 - 128 * (w % 2)), (384, 256, 128))
    ]
    crossed = []
    for i, (w, start, size, _) in enumerate(items):
        if i % 2 == 0:
            (l_i, l_s, l_o)[w].wait()
        piece = quarter(w, x_hi, second, on_color(second, y, z), start, size)
        crossed.append(send(piece, piece, cross))
        if i == 1:
            own_bias = IB.at[:, part(x_hi, PAD)]
            b_crossed = send(own_bias, own_bias, cross)

    for W in weights:
        for j in range(2):
            W[pl.ds(j * PAD + SHARD, PAD - SHARD), :] = jnp.zeros((PAD - SHARD, D), BF16)

    def one_hot_sel(k):
        def body(i, _):
            h = lax.broadcasted_iota(jnp.int32, (128, D), 0) + i * 128
            col = lax.broadcasted_iota(jnp.int32, (128, D), 1)
            hi = (h >= PAD).astype(jnp.int32)
            j = h - hi * PAD
            want = hi * 640 + k * SHARD + j
            sel[part(i, 128), :] = jnp.where((col == want) & (j < SHARD), 1.0, 0.0).astype(BF16)
            return 0

        lax.fori_loop(0, HALF // 128, body, 0)

    beside_of, own_of, relayed = {}, {}, {}

    def forward_first(i):
        w, start, size, _ = items[i]
        q, up, down = ring(first)
        crossed[i].wait_recv()
        piece = quarter(w, other_hi, first, q, start, size)
        beside_of[i] = send(piece, piece, beside)
        own_of[i, 0] = send(piece, piece, up), send(piece, piece, down)

    def forward_second(i):
        w, start, size, _ = items[i]
        q, up, down = ring(second)
        beside_of[i].wait_recv()
        piece = quarter(w, other_hi, second, q, start, size)
        own_of[i, 1] = send(piece, piece, up), send(piece, piece, down)

    def relay(i, turn):
        w, start, size, cut = items[i]
        color = (first, second)[turn]
        q, up, down = ring(color)
        from_below, from_above = own_of[i, turn]
        from_below.wait_recv()
        a = quarter(w, other_hi, color, rem(q + 3, 4), start, cut)
        s1 = send(a, a, up)
        from_above.wait_recv()
        b = quarter(w, other_hi, color, rem(q + 1, 4), start + cut, size - cut)
        relayed[i, turn] = s1, send(b, b, down)

    def arrived(i):
        for turn in range(2):
            for c in relayed[i, turn]:
                c.wait_recv()

    def sel_body(i, _):
        sH[:, part(i, 256)] = mm(S[...], sel[part(i, 256), :], NT).astype(BF16)
        return 0

    def make_perm(k):
        def body(i, _):
            n = lax.broadcasted_iota(jnp.int32, (128, 128), 0) + i * 128
            want = natural(n, ORDERS[k])
            lane = lax.broadcasted_iota(jnp.int32, (128, 128), 1)
            for t in range(HALF // 128):
                perm[k, part(i, 128), pl.ds(t * 128, 128)] = jnp.where(
                    lane + t * 128 == want, 1.0, 0.0
                ).astype(BF16)
            return 0

        lax.fori_loop(0, OWN // 128, body, 0)

    def transposed(k, src):
        def body(i, _):
            LT[k, :, part(i, 256)] = mm(perm[k], src[part(i, 256), :], NT).astype(BF16)
            return 0

        lax.fori_loop(0, CHIP // 256, body, 0)

    def spread_body(i, _):
        cols = part(i, 256)
        col = lax.broadcasted_iota(jnp.int32, (128, 256), 1) + i * 256
        row = lax.broadcasted_iota(jnp.int32, (128, 256), 0)
        off = col - row * QUANTILES
        spreader = jnp.where((off >= 0) & (off < QUANTILES), 1.0, 0.0).astype(F32)
        spread[:, cols] = (
            lax.dot_general(
                T[...], spreader, NN, precision=lax.Precision.HIGHEST, preferred_element_type=F32
            )
            - p_own[:1, cols]
        )
        rows = jnp.zeros((128, 256), F32)
        for c in range(QUANTILES):
            level = jnp.full((128, 256), levels_ref[c], jnp.int32).astype(F32) + 1.0
            rows = rows + jnp.where(off == c, level / (LEVELS + 1), 0.0)
        tau[:, cols] = jnp.sum(rows, axis=0, keepdims=True)
        return 0

    def hidden_body(i, _):
        cols = part(i, 256)
        pre = mm(S[...], Wi[cols, :], NT) + IB[:, cols]
        sig = jax.nn.sigmoid(pre)
        H[:, cols] = (pre * sig).astype(BF16)
        DV[:, cols] = sig * (1.0 + pre * (1.0 - sig))
        return 0

    def isel_body(dst):
        def body(i, _):
            dst[:, part(i, 256)] = mm(sel[...], Wi[part(i, 256), :], NT).astype(BF16)
            return 0

        lax.fori_loop(0, HALF // 256, body, 0)

    one_hot_sel(core)
    l_series.wait()
    p_own[:1, :] = ob_ref[...].reshape(1, D)
    lax.fori_loop(0, 3, sel_body, 0)
    forward_first(0)
    make_perm(0)
    forward_first(1)
    make_perm(1)
    forward_first(2)
    make_perm(2)
    forward_first(3)
    forward_second(0)
    relay(0, 0)
    transposed(0, sH)
    forward_first(4)
    forward_second(1)
    relay(1, 0)
    l_t.wait()
    lax.fori_loop(0, 2, spread_body, 0)
    forward_first(5)
    forward_second(2)
    relay(2, 0)
    lax.fori_loop(2, 5, spread_body, 0)
    forward_second(3)
    relay(3, 0)
    relay(0, 1)
    forward_second(4)
    relay(4, 0)
    relay(1, 1)
    forward_second(5)
    relay(5, 0)
    relay(2, 1)
    arrived(0)
    arrived(1)
    b_crossed.wait_recv()
    relay(3, 1)
    lax.fori_loop(0, 2, hidden_body, 0)
    relay(4, 1)
    lax.fori_loop(2, 3, hidden_body, 0)
    relay(5, 1)
    transposed(1, H)
    isel_body(isel.at[core])
    for i in range(2, 6):
        arrived(i)

    mine, theirs = part(core, CORE), part(1 - core, CORE)

    def predict(rows, cols):
        return mm(H[rows, :], Wo[:, cols]) + mm(sH[rows, :], Ws[:, cols])

    p_copies = []
    for i in range(D // 256):
        cols = pl.ds(i * 256, 256)
        p_send[i] = predict(theirs, cols)
        p_copies.append(send(p_send.at[i], p_recv.at[i], partner))

    def predict_body(i, _):
        cols = part(i, 256)
        p_own[:, cols] = predict(mine, cols)
        return 0

    lax.fori_loop(0, D // 256, predict_body, 0)
    for c in p_copies:
        c.wait_recv()

    def slope_body(w, _):
        rows = part(w, PATCHES)
        count = counts_ref[(x_hi * 2 + core) * (CORE // PATCHES) + w]
        counted = jnp.full((PATCHES, 128), count, jnp.int32)
        valid = lax.broadcasted_iota(jnp.int32, (PATCHES, 128), 0) < counted
        weight = (jnp.where(valid, 1.0, 0.0) / counted.astype(F32))[:, :1]
        for i in range(D // 256):
            cols = pl.ds(i * 256, 256)
            residue = spread[rows, cols] - (p_own[rows, cols] + p_recv[i, rows, :])
            t = tau[:, cols]
            slopes = jnp.where(residue >= 0, t, 1.0 - t) * jnp.clip(
                residue / HUBER_WIDTH, -1.0, 1.0
            )
            OG[pl.ds(pl.multiple_of(core * CORE + w * PATCHES, PATCHES), PATCHES), cols] = (
                -slopes * weight
            ).astype(BF16)
        return 0

    og_copies = []
    for i in range(2):
        lax.fori_loop(8 * i, 8 * i + 8, slope_body, 0)
        rows = OG.at[part(core * 2 + i, 128), :]
        og_copies.append(send(rows, rows, partner))

    def backflow(rows):
        def body(i, _):
            cols = part(i, 256)
            back = mm(OG[rows, :], Wo[cols, :], NT)
            HG[core, rows, cols] = (back * DV[rows, cols]).astype(BF16)
            return 0

        lax.fori_loop(0, HALF // 256, body, 0)

    backflow(mine)
    for c in og_copies:
        c.wait_recv()

    def halves(h):
        return pl.ds(h * LANES, LANES)

    def ring_start(axis, view, ra, rd):
        p = pos[axis]
        up, down = along(axis, 1), along(axis, 3)
        return (
            send(view(rem(p + 2, 4), 0), ra.at[0], up),
            send(view(rem(p + 2, 4), 1), ra.at[1], down),
            send(view(rem(p + 1, 4), 1), rd.at[0], up),
            send(view(rem(p + 3, 4), 0), rd.at[1], down),
        )

    def ring_pass(axis, size, rows, own, ra, out, rsum, step):
        p = pos[axis]
        passed = []
        for h, hop in ((0, 1), (1, 3)):
            step[h].wait_recv()

            def body(i, _, h=h, hop=hop):
                there = pl.ds(pl.multiple_of(rem(p + hop, 4) * size + i * rows, 8), rows)
                here = part(i, rows)
                out[h, here, :] = (
                    own[there, halves(h)] + ra[h, here, :].astype(F32)
                ).astype(BF16)
                return 0

            lax.fori_loop(0, size // rows, body, 0)
            passed.append(send(out.at[h], rsum.at[h], along(axis, hop)))
        return passed

    def ring_end(axis, size, rows, own, rsum, rd, dst, step, passed):
        p = pos[axis]
        for c in (step[2], step[3], passed[0], passed[1]):
            c.wait_recv()

        def body(i, _):
            there = pl.ds(pl.multiple_of(p * size + i * rows, 8), rows)
            here = part(i, rows)
            for h in range(2):
                dst[here, halves(h)] = (
                    own[there, halves(h)]
                    + rsum[h, here, :].astype(F32)
                    + rd[1 - h, here, :].astype(F32)
                )
            return 0

        lax.fori_loop(0, size // rows, body, 0)

    def gradient(k, right):
        def body(i, _):
            cols = part(i, 256)
            g = mm(LT[k], right[:, cols])
            G[k, :, cols] = g
            ST[k, :, cols] = g.astype(BF16)
            return 0

        lax.fori_loop(0, D // 256, body, 0)
        return ring_start(
            ORDERS[k][0], lambda q, h: ST.at[k, part(q, C1), halves(h)], RA.at[k], RD.at[k]
        )

    def pass_on(k, step):
        return ring_pass(
            ORDERS[k][0], C1, 32, G.at[k], RA.at[k], T2.at[k], RSUM.at[k], step
        )

    def second_phase(k, step, passed):
        ring_end(ORDERS[k][0], C1, 32, G.at[k], RSUM.at[k], RD.at[k], acc1.at[k], step, passed)
        for q in range(4):
            ST2[k, q] = acc1[k, pl.ds(q * C2, C2), :].astype(BF16)
        return ring_start(
            ORDERS[k][1], lambda q, h: ST2.at[k, q, :, halves(h)], RA2.at[k], RD2.at[k]
        )

    def pass_on_second(k, step):
        return ring_pass(
            ORDERS[k][1], C2, C2, acc1.at[k], RA2.at[k], T3.at[k], RSUM2.at[k], step
        )

    def third_phase(k, step, passed):
        ring_end(
            ORDERS[k][1], C2, C2, acc1.at[k], RSUM2.at[k], RD2.at[k], acc2.at[k], step, passed
        )
        for q in range(4):
            piece = acc2[k, pl.ds(q * C3, C3), :]
            F3[k, q] = piece
            ST3[k, q] = piece.astype(BF16)
        axis = ORDERS[k][2]
        p3 = pos[axis]
        return [send(ST3.at[k, rem(p3 + o, 4)], R3.at[k, o - 1], along(axis, o)) for o in (1, 3, 2)]

    rescale = 1.0 / 2048

    def finish(k, step, out):
        p3 = pos[ORDERS[k][2]]
        for c in step:
            c.wait_recv()
        total = F3[k, p3]
        for o in range(3):
            total = total + R3[k, o].astype(F32)
        out[...] = total * rescale

    skip1 = gradient(0, OG)
    backflow(theirs)
    hg_copy = send(HG.at[core], HG.at[core], partner)
    transposed(2, HG.at[core])
    inner1 = gradient(2, S)
    outer1 = gradient(1, OG)

    bsend[0, :, pl.ds(0, HALF)] = jnp.sum(HG[core].astype(F32), axis=0, keepdims=True)
    bsend[0, :, pl.ds(HALF, D)] = jnp.sum(OG[...].astype(F32), axis=0, keepdims=True)

    def bias_send(i):
        axis = "xyz"[i]
        return [send(bsend.at[i], brecv.at[i, o - 1], along(axis, o)) for o in (1, 2, 3)]

    def bias_add(i, copies):
        for c in copies:
            c.wait_recv()
        bsend[i + 1] = bsend[i] + brecv[i, 0] + brecv[i, 1] + brecv[i, 2]

    bias1 = bias_send(0)
    one_hot_sel(1 - core)
    skip2 = pass_on(0, skip1)
    isel_body(isel_send)
    isel_copy = send(isel_send, isel.at[core], partner)
    inner2 = pass_on(2, inner1)
    hg_copy.wait_recv()
    isel_copy.wait_recv()

    def input_body(i, _):
        rows = part(i, 256)
        igf[:, rows] = (
            mm(isel[0], HG[0, rows, :], NT)
            + mm(isel[1], HG[1, rows, :], NT)
            + mm(Ws[...], OG[rows, :], NT)
        )
        return 0

    lax.fori_loop(0, CHIP // 256, input_body, 0)
    ig_send[...] = igf[pl.ds(pl.multiple_of(other_hi * PAD, 128), SHARD), :].astype(BF16)
    lower, upper = pl.ds(0, SHARD // 2), pl.ds(SHARD // 2, SHARD // 2)
    ig1 = (
        send(ig_send.at[lower, :], ig_mid.at[lower, :], along("x", 1)),
        send(ig_send.at[upper, :], ig_mid.at[upper, :], along("x", 3)),
    )
    out0 = pltpu.make_async_copy(
        igf.at[own_rows, :], in_out.at[:, part(x_hi, CHIP)], lsem.at[len(loads)]
    )
    out0.start()
    outer2 = pass_on(1, outer1)
    bias_add(0, bias1)
    bias2 = bias_send(1)
    skip3 = second_phase(0, skip1, skip2)
    for c in ig1:
        c.wait_recv()
    ig2 = (
        send(ig_mid.at[lower, :], ig_recv.at[lower, :], along("x", 1)),
        send(ig_mid.at[upper, :], ig_recv.at[upper, :], along("x", 3)),
    )
    inner3 = second_phase(2, inner1, inner2)
    skip4 = pass_on_second(0, skip3)
    outer3 = second_phase(1, outer1, outer2)
    bias_add(1, bias2)
    bias3 = bias_send(2)
    inner4 = pass_on_second(2, inner3)
    skip5 = third_phase(0, skip3, skip4)
    outer4 = pass_on_second(1, outer3)
    for c in ig2:
        c.wait_recv()
    outs[...] = ig_recv[...].astype(F32)
    out1 = pltpu.make_async_copy(
        outs, in_out.at[:, part(other_hi, CHIP)], lsem.at[len(loads) + 1]
    )
    out1.start()
    inner5 = third_phase(2, inner3, inner4)
    outer5 = third_phase(1, outer3, outer4)
    bias_add(2, bias3)

    def pick(v, start):
        n = v.shape[1]
        i = lax.broadcasted_iota(jnp.int32, (n, 128), 0)
        j = lax.broadcasted_iota(jnp.int32, (n, 128), 1)
        hot = jnp.where(i == j + start, 1.0, 0.0).astype(F32)
        return lax.dot_general(
            jnp.broadcast_to(v, (8, n)), hot, NN,
            precision=lax.Precision.HIGHEST, preferred_element_type=F32,
        )[:1] * rescale

    ib_out[...] = pick(bsend[3, :, pl.ds(0, HALF)], x_hi * PAD + dp * 10)[:, :10]
    ob_out[...] = pick(bsend[3, :, pl.ds(HALF, D)], dp * 40)[:, :40]
    finish(0, skip5, gs_out)
    finish(2, inner5, gi_out)
    finish(1, outer5, go_out)
    for c in sent:
        c.wait_send()
    out0.wait()
    out1.wait()


N_SENDS = 136


def write_out(*refs):
    ins, outs, (big, grads, b10, b40, sem_in, sem_out) = refs[:6], refs[6:12], refs[12:]
    hops = [
        (ins[0].at[part(i, 80), :], big.at[part(i, 80), :], outs[0].at[part(i, 80), :])
        for i in range(4)
    ]
    hops += [(ins[i], grads.at[i - 1], outs[i]) for i in (1, 2, 3)]
    hops += [(ins[4], b10, outs[4]), (ins[5], b40, outs[5])]
    copies = []
    for i, (src, mid, dst) in enumerate(hops):
        c = pltpu.make_async_copy(src, mid, sem_in.at[i])
        c.start()
        copies.append((c, pltpu.make_async_copy(mid, dst, sem_out.at[i])))
    for a, b in copies:
        a.wait()
        b.start()
    for _, b in copies:
        b.wait()


def on_device(series, wi, ib, wo, ws, ob, targets, levels, counts):
    hbm = pl.BlockSpec(memory_space=pl.ANY)
    vmem = pl.BlockSpec(memory_space=pltpu.VMEM)
    smem = pl.BlockSpec(memory_space=pltpu.SMEM)
    grad = jax.ShapeDtypeStruct((C3, D), F32)
    shapes = (
        jax.ShapeDtypeStruct((SHARD, 2 * CHIP), F32), grad, grad, grad,
        jax.ShapeDtypeStruct((1, 10), F32), jax.ShapeDtypeStruct((1, 40), F32),
    )
    results = pl.pallas_call(
        kernel,
        out_shape=shapes,
        in_specs=[hbm] * 4 + [vmem] * 2 + [hbm] + [smem] * 2,
        out_specs=(hbm,) + (vmem,) * 5,
        scratch_shapes=[
            pltpu.VMEM((CHIP, D), BF16),
            pltpu.VMEM((HALF, D), BF16),
            pltpu.VMEM((HALF, D), BF16),
            pltpu.VMEM((HALF, D), BF16),
            pltpu.VMEM((1, HALF), F32),
            pltpu.VMEM((CORE, 128), F32),
            pltpu.VMEM((HALF, D), BF16),
            pltpu.VMEM((3, OWN, HALF), BF16),
            pltpu.VMEM((2, HALF, HALF), BF16),
            pltpu.VMEM((HALF, HALF), BF16),
            pltpu.VMEM((CHIP, HALF), BF16),
            pltpu.VMEM((CHIP, HALF), BF16),
            pltpu.VMEM((CHIP, HALF), F32),
            pltpu.VMEM((3, OWN, CHIP), BF16),
            pltpu.VMEM((2, CHIP, HALF), BF16),
            pltpu.VMEM((CHIP, D), BF16),
            pltpu.VMEM((CORE, D), F32),
            pltpu.VMEM((1, D), F32),
            pltpu.VMEM((5, CORE, 256), F32),
            pltpu.VMEM((5, CORE, 256), F32),
            pltpu.VMEM((CORE, D), F32),
            pltpu.VMEM((3, OWN, D), F32),
            pltpu.VMEM((3, OWN, D), BF16),
            pltpu.VMEM((3, 2, C1, LANES), BF16),
            pltpu.VMEM((3, 2, C1, LANES), BF16),
            pltpu.VMEM((3, 2, C1, LANES), BF16),
            pltpu.VMEM((3, 2, C1, LANES), BF16),
            pltpu.VMEM((3, C1, D), F32),
            pltpu.VMEM((3, 4, C2, D), BF16),
            pltpu.VMEM((3, 2, C2, LANES), BF16),
            pltpu.VMEM((3, 2, C2, LANES), BF16),
            pltpu.VMEM((3, 2, C2, LANES), BF16),
            pltpu.VMEM((3, 2, C2, LANES), BF16),
            pltpu.VMEM((3, C2, D), F32),
            pltpu.VMEM((3, 4, C3, D), F32),
            pltpu.VMEM((3, 4, C3, D), BF16),
            pltpu.VMEM((3, 3, C3, D), BF16),
            pltpu.VMEM((4, 1, HALF + D), F32),
            pltpu.VMEM((3, 3, 1, HALF + D), F32),
            pltpu.VMEM((HALF, CHIP), F32),
            pltpu.VMEM((SHARD, CHIP), BF16),
            pltpu.VMEM((SHARD, CHIP), BF16),
            pltpu.VMEM((SHARD, CHIP), BF16),
            pltpu.VMEM((SHARD, CHIP), F32),
            pltpu.SemaphoreType.DMA((8,)),
            pltpu.SemaphoreType.DMA((N_SENDS,)),
            pltpu.SemaphoreType.DMA((N_SENDS,)),
        ],
        compiler_params=pltpu.CompilerParams(
            collective_id=0, has_side_effects=True, vmem_limit_bytes=60 * 1024 * 1024
        ),
    )(series, wi, wo, ws, ib, ob, targets, levels, counts)
    input_grad, inner, outer, skip, inbias, outbias = pl.pallas_call(
        write_out,
        out_shape=shapes,
        in_specs=[hbm] * 6,
        out_specs=(hbm,) * 6,
        scratch_shapes=[
            pltpu.VMEM((SHARD, 2 * CHIP), F32),
            pltpu.VMEM((3, C3, D), F32),
            pltpu.VMEM((1, 10), F32),
            pltpu.VMEM((1, 40), F32),
            pltpu.SemaphoreType.DMA((9,)),
            pltpu.SemaphoreType.DMA((9,)),
        ],
    )(*results)
    return input_grad.T, inner, outer, skip, inbias.reshape(10), outbias.reshape(40)


def solution(mesh):
    return jax.shard_map(
        on_device,
        mesh=mesh,
        in_specs=(
            P("dp", None), P("mp", None), P("mp"), P("mp", None), P("mp", None), P(None),
            P("dp", None), P(None), P("dp"),
        ),
        out_specs=(
            P("dp", "mp"), P(("mp", "dp"), None), P(("mp", "dp"), None), P(("mp", "dp"), None),
            P(("mp", "dp")), P("dp"),
        ),
        check_vma=False,
    )
```

time: 92.6 us -> 82.6 us (0.89)
  local copies, waits for them, and re-layouts: 8.49 us -> 0 us
    unnamed x16 -> x0, local copies, waits for them, and re-layouts: 5.94 us -> none
    reshape x2 -> x0, local copies, waits for them, and re-layouts: 1.86 us -> none  [the longest x1 1.29 us: on_device(): ob.reshape(1, D)]
    pallas_call x1 -> x2, Pallas kernels: 82.3 us -> 81.8 us  [the longest x1 79.5 us: on_device(): pl.pallas_call(kernel, out_shape=shapes, in_specs=[hbm] * 4 + [vmem] * 2...]
where the time goes in v2:
time: 82.6 us; the launch traced here: 82.4 us
  Pallas kernels  81.8 us (99%)
    pallas_call x1, Pallas kernels, on_device(): pl.pallas_call(kernel, out_shape=shapes, in_specs=[hbm] * 4 + [vmem] * 2...  79.5 us
    pallas_call x1, Pallas kernels, on_device(): pl.pallas_call(write_out, out_shape=shapes, in_specs=[hbm] * 6, out_specs...  2.26 us

profile of v2, /device:TPU:0, one launch (start us, length us, event | category | flops | bytes accessed | tf_op | source)
XLA Modules:
  0.0 82.4 jit_solution(850819905899906370)
XLA Ops:
  0.6 79.5 %shard_map.136 = (f32[320,1024]{1,0:T(8,128)}, f32[10,1280]{1,0:T(8,128)}, f32[10,1280]{1,0:T(8,128)}, f32[10,1280]{1,0:T(8,128)}, f32[1,10]{1,0:T(1,128)}, /*index=5*/f32[1,40]{1,0:T(1,128)}) custom-call(bf16[1024,1280]{1,0:T(8,128)(2,1)} %series_hbm.1, bf16[320,1280]{1,0:T(8,128)(2,1)} %wi_hbm.1, bf16[320,1280]{1,0:T(8,128)(2,1)} %wo_hbm.1, ...), custom_call_target="tpu_custom_call" | custom-call | tf_op jit(solution)/shard_map/pallas_call | solution.py:614
  80.2 2.3 %shard_map.137 = (f32[320,1024]{1,0:T(8,128)}, f32[10,1280]{1,0:T(8,128)}, f32[10,1280]{1,0:T(8,128)}, f32[10,1280]{1,0:T(8,128)}, f32[1,10]{1,0:T(1,128)}, /*index=5*/f32[1,40]{1,0:T(1,128)}) custom-call(f32[320,1024]{1,0:T(8,128)} %get-tuple-element.18.refs_0_, f32[10,1280]{1,0:T(8,128)} %get-tuple-element.19.refs_1_, ...), custom_call_target="tpu_custom_call" | custom-call | tf_op jit(solution)/shard_map/pallas_call | solution.py:672

commit v3 on v2

--- a/solution.py
+++ b/solution.py
@@ -25,6 +25,7 @@
 
 NN = (((1,), (0,)), ((), ()))
 NT = (((1,), (1,)), ((), ()))
+TT = (((0,), (1,)), ((), ()))
 
 
 def mm(a, b, dims=NN):
@@ -43,7 +44,7 @@
     return pl.ds(pl.multiple_of(index * size, size), size)
 
 
-ORDERS = ("xyz", "yzx", "zyx")
+GROUPS = (("yxz", 0, 256), ("zyx", 512, 256), ("xzy", 1024, 128))
 
 
 def split(n, size):
@@ -68,10 +69,10 @@
 def kernel(
     series_hbm, wi_hbm, wo_hbm, ws_hbm, ib_ref, ob_ref, targets_hbm, levels_ref, counts_ref,
     in_out, gi_out, go_out, gs_out, ib_out, ob_out,
-    S, Wi, Wo, Ws, IB, T, sel, perm, isel, isel_send, sH, H, DV, LT, HG, OG,
+    S, Wi, Wo, Ws, IB, T, sel, perm, sH, H, DV, LT, HG, OG,
     spread, tau, p_send, p_recv, p_own, G, ST, RA, RD, RSUM, T2,
     acc1, ST2, RA2, RD2, RSUM2, T3, acc2, F3, ST3, R3,
-    bsend, brecv, igf, ig_send, ig_mid, ig_recv, outs,
+    bsend, brecv, igp, igp_recv, igf, ig_send, ig_mid, ig_recv,
     lsem, ssem, rsem,
 ):
     dp = lax.axis_index("dp")
@@ -158,12 +159,15 @@
         for w in range(3)
         for start, size, cut in ((0, 384, 256 - 128 * (w % 2)), (384, 256, 128))
     ]
-    crossed = []
+    crossed, beside_of, own_of, relayed = [], {}, {}, {}
     for i, (w, start, size, _) in enumerate(items):
         if i % 2 == 0:
             (l_i, l_s, l_o)[w].wait()
         piece = quarter(w, x_hi, second, on_color(second, y, z), start, size)
         crossed.append(send(piece, piece, cross))
+        if w == 2:
+            piece = quarter(w, x_hi, first, on_color(first, y, z), start, size)
+            beside_of[i] = send(piece, piece, cross)
         if i == 1:
             own_bias = IB.at[:, part(x_hi, PAD)]
             b_crossed = send(own_bias, own_bias, cross)
@@ -184,14 +188,13 @@
 
         lax.fori_loop(0, HALF // 128, body, 0)
 
-    beside_of, own_of, relayed = {}, {}, {}
-
     def forward_first(i):
         w, start, size, _ = items[i]
         q, up, down = ring(first)
         crossed[i].wait_recv()
         piece = quarter(w, other_hi, first, q, start, size)
-        beside_of[i] = send(piece, piece, beside)
+        if w < 2:
+            beside_of[i] = send(piece, piece, beside)
         own_of[i, 0] = send(piece, piece, up), send(piece, piece, down)
 
     def forward_second(i):
@@ -225,7 +228,7 @@
     def make_perm(k):
         def body(i, _):
             n = lax.broadcasted_iota(jnp.int32, (128, 128), 0) + i * 128
-            want = natural(n, ORDERS[k])
+            want = natural(n, GROUPS[k][0])
             lane = lax.broadcasted_iota(jnp.int32, (128, 128), 1)
             for t in range(HALF // 128):
                 perm[k, part(i, 128), pl.ds(t * 128, 128)] = jnp.where(
@@ -235,12 +238,12 @@
 
         lax.fori_loop(0, OWN // 128, body, 0)
 
-    def transposed(k, src):
+    def transposed(k, g, src):
         def body(i, _):
-            LT[k, :, part(i, 256)] = mm(perm[k], src[part(i, 256), :], NT).astype(BF16)
+            LT[k, g, :, part(i, 256)] = mm(perm[g], src[part(i, 256), :], NT).astype(BF16)
             return 0
 
-        lax.fori_loop(0, CHIP // 256, body, 0)
+        lax.fori_loop(0, CHIP // 256, body, 0, unroll=True)
 
     def spread_body(i, _):
         cols = part(i, 256)
@@ -269,13 +272,6 @@
         DV[:, cols] = sig * (1.0 + pre * (1.0 - sig))
         return 0
 
-    def isel_body(dst):
-        def body(i, _):
-            dst[:, part(i, 256)] = mm(sel[...], Wi[part(i, 256), :], NT).astype(BF16)
-            return 0
-
-        lax.fori_loop(0, HALF // 256, body, 0)
-
     one_hot_sel(core)
     l_series.wait()
     p_own[:1, :] = ob_ref[...].reshape(1, D)
@@ -289,7 +285,7 @@
     forward_first(3)
     forward_second(0)
     relay(0, 0)
-    transposed(0, sH)
+    transposed(0, 0, sH)
     forward_first(4)
     forward_second(1)
     relay(1, 0)
@@ -302,22 +298,23 @@
     forward_second(3)
     relay(3, 0)
     relay(0, 1)
+    transposed(0, 1, sH)
     forward_second(4)
     relay(4, 0)
     relay(1, 1)
     forward_second(5)
     relay(5, 0)
     relay(2, 1)
+    transposed(0, 2, sH)
     arrived(0)
     arrived(1)
     b_crossed.wait_recv()
     relay(3, 1)
-    lax.fori_loop(0, 2, hidden_body, 0)
+    lax.fori_loop(0, 2, hidden_body, 0, unroll=True)
     relay(4, 1)
     lax.fori_loop(2, 3, hidden_body, 0)
     relay(5, 1)
-    transposed(1, H)
-    isel_body(isel.at[core])
+    transposed(1, 0, H)
     for i in range(2, 6):
         arrived(i)
 
@@ -337,7 +334,9 @@
         p_own[:, cols] = predict(mine, cols)
         return 0
 
-    lax.fori_loop(0, D // 256, predict_body, 0)
+    lax.fori_loop(0, D // 256, predict_body, 0, unroll=True)
+    transposed(1, 1, H)
+    transposed(1, 2, H)
     for c in p_copies:
         c.wait_recv()
 
@@ -369,126 +368,156 @@
         def body(i, _):
             cols = part(i, 256)
             back = mm(OG[rows, :], Wo[cols, :], NT)
-            HG[core, rows, cols] = (back * DV[rows, cols]).astype(BF16)
+            HG[rows, cols] = (back * DV[rows, cols]).astype(BF16)
             return 0
 
-        lax.fori_loop(0, HALF // 256, body, 0)
+        lax.fori_loop(0, HALF // 256, body, 0, unroll=True)
 
     backflow(mine)
     for c in og_copies:
         c.wait_recv()
 
-    def halves(h):
-        return pl.ds(h * LANES, LANES)
-
-    def ring_start(axis, view, ra, rd):
+    def lanes(g, h):
+        return pl.ds(GROUPS[g][1] + h * GROUPS[g][2], GROUPS[g][2])
+
+    def half_lanes(g):
+        return pl.ds(GROUPS[g][1] // 2, GROUPS[g][2])
+
+    def ring_start(axis, g, view, ra, rd):
         p = pos[axis]
         up, down = along(axis, 1), along(axis, 3)
+        to = half_lanes(g)
         return (
-            send(view(rem(p + 2, 4), 0), ra.at[0], up),
-            send(view(rem(p + 2, 4), 1), ra.at[1], down),
-            send(view(rem(p + 1, 4), 1), rd.at[0], up),
-            send(view(rem(p + 3, 4), 0), rd.at[1], down),
+            send(view(rem(p + 2, 4), lanes(g, 0)), ra.at[0, :, to], up),
+            send(view(rem(p + 2, 4), lanes(g, 1)), ra.at[1, :, to], down),
+            send(view(rem(p + 1, 4), lanes(g, 1)), rd.at[0, :, to], up),
+            send(view(rem(p + 3, 4), lanes(g, 0)), rd.at[1, :, to], down),
         )
 
-    def ring_pass(axis, size, rows, own, ra, out, rsum, step):
+    def ring_pass(axis, g, size, rows, base, ra, out, rsum, own, step):
         p = pos[axis]
+        to = half_lanes(g)
         passed = []
         for h, hop in ((0, 1), (1, 3)):
             step[h].wait_recv()
 
             def body(i, _, h=h, hop=hop):
-                there = pl.ds(pl.multiple_of(rem(p + hop, 4) * size + i * rows, 8), rows)
+                there = pl.ds(
+                    pl.multiple_of(base + rem(p + hop, 4) * size + i * rows, 8), rows
+                )
                 here = part(i, rows)
-                out[h, here, :] = (
-                    own[there, halves(h)] + ra[h, here, :].astype(F32)
+                out[h, here, to] = (
+                    own[there, lanes(g, h)] + ra[h, here, to].astype(F32)
                 ).astype(BF16)
                 return 0
 
             lax.fori_loop(0, size // rows, body, 0)
-            passed.append(send(out.at[h], rsum.at[h], along(axis, hop)))
+            passed.append(send(out.at[h, :, to], rsum.at[h, :, to], along(axis, hop)))
         return passed
 
-    def ring_end(axis, size, rows, own, rsum, rd, dst, step, passed):
+    def ring_end(axis, g, size, rows, base, rsum, rd, own, dst, step, passed):
         p = pos[axis]
+        to = half_lanes(g)
         for c in (step[2], step[3], passed[0], passed[1]):
             c.wait_recv()
 
         def body(i, _):
-            there = pl.ds(pl.multiple_of(p * size + i * rows, 8), rows)
+            there = pl.ds(pl.multiple_of(base + p * size + i * rows, 8), rows)
             here = part(i, rows)
             for h in range(2):
-                dst[here, halves(h)] = (
-                    own[there, halves(h)]
-                    + rsum[h, here, :].astype(F32)
-                    + rd[1 - h, here, :].astype(F32)
+                dst[here, lanes(g, h)] = (
+                    own[there, lanes(g, h)]
+                    + rsum[h, here, to].astype(F32)
+                    + rd[1 - h, here, to].astype(F32)
                 )
             return 0
 
         lax.fori_loop(0, size // rows, body, 0)
 
+    steps = {}
+
     def gradient(k, right):
-        def body(i, _):
-            cols = part(i, 256)
-            g = mm(LT[k], right[:, cols])
-            G[k, :, cols] = g
-            ST[k, :, cols] = g.astype(BF16)
-            return 0
-
-        lax.fori_loop(0, D // 256, body, 0)
-        return ring_start(
-            ORDERS[k][0], lambda q, h: ST.at[k, part(q, C1), halves(h)], RA.at[k], RD.at[k]
-        )
-
-    def pass_on(k, step):
-        return ring_pass(
-            ORDERS[k][0], C1, 32, G.at[k], RA.at[k], T2.at[k], RSUM.at[k], step
-        )
-
-    def second_phase(k, step, passed):
-        ring_end(ORDERS[k][0], C1, 32, G.at[k], RSUM.at[k], RD.at[k], acc1.at[k], step, passed)
-        for q in range(4):
-            ST2[k, q] = acc1[k, pl.ds(q * C2, C2), :].astype(BF16)
-        return ring_start(
-            ORDERS[k][1], lambda q, h: ST2.at[k, q, :, halves(h)], RA2.at[k], RD2.at[k]
-        )
-
-    def pass_on_second(k, step):
-        return ring_pass(
-            ORDERS[k][1], C2, C2, acc1.at[k], RA2.at[k], T3.at[k], RSUM2.at[k], step
-        )
-
-    def third_phase(k, step, passed):
-        ring_end(
-            ORDERS[k][1], C2, C2, acc1.at[k], RSUM2.at[k], RD2.at[k], acc2.at[k], step, passed
-        )
-        for q in range(4):
-            piece = acc2[k, pl.ds(q * C3, C3), :]
-            F3[k, q] = piece
-            ST3[k, q] = piece.astype(BF16)
-        axis = ORDERS[k][2]
-        p3 = pos[axis]
-        return [send(ST3.at[k, rem(p3 + o, 4)], R3.at[k, o - 1], along(axis, o)) for o in (1, 3, 2)]
+        for g, (order, start, width) in enumerate(GROUPS):
+            def body(i, _, g=g):
+                cols = part(i, 256)
+                value = mm(LT[k, g], right[:, cols])
+                G[k, :, cols] = value
+                ST[k, :, cols] = value.astype(BF16)
+                return 0
+
+            lax.fori_loop(start // 256, (start + 2 * width) // 256, body, 0, unroll=True)
+            steps[k, g, 0] = ring_start(
+                order[0], g, lambda q, cols: ST.at[k, part(q, C1), cols], RA.at[k], RD.at[k]
+            )
+
+    def pass_on(k):
+        for g, (order, _, _) in enumerate(GROUPS):
+            steps[k, g, 1] = ring_pass(
+                order[0], g, C1, 32, 0, RA.at[k], T2.at[k], RSUM.at[k], G.at[k], steps[k, g, 0]
+            )
+
+    def second_phase(k):
+        for g, (order, start, width) in enumerate(GROUPS):
+            ring_end(
+                order[0], g, C1, 32, 0, RSUM.at[k], RD.at[k], G.at[k], acc1.at[k],
+                steps[k, g, 0], steps[k, g, 1],
+            )
+            cols = pl.ds(start, 2 * width)
+            for q in range(4):
+                ST2[k, q, :, cols] = acc1[k, pl.ds(q * C2, C2), cols].astype(BF16)
+            steps[k, g, 2] = ring_start(
+                order[1], g, lambda q, cols: ST2.at[k, q, :, cols], RA2.at[k], RD2.at[k]
+            )
+
+    def pass_on_second(k):
+        for g, (order, _, _) in enumerate(GROUPS):
+            steps[k, g, 3] = ring_pass(
+                order[1], g, C2, C2, 0, RA2.at[k], T3.at[k], RSUM2.at[k], acc1.at[k],
+                steps[k, g, 2],
+            )
+
+    def third_phase(k):
+        for g, (order, start, width) in enumerate(GROUPS):
+            ring_end(
+                order[1], g, C2, C2, 0, RSUM2.at[k], RD2.at[k], acc1.at[k], acc2.at[k],
+                steps[k, g, 2], steps[k, g, 3],
+            )
+            cols = pl.ds(start, 2 * width)
+            for q in range(4):
+                piece = acc2[k, pl.ds(q * C3, C3), cols]
+                F3[k, q, :, cols] = piece
+                ST3[k, q, :, cols] = piece.astype(BF16)
+            p3 = pos[order[2]]
+            steps[k, g, 4] = [
+                send(
+                    ST3.at[k, rem(p3 + o, 4), :, cols], R3.at[k, o - 1, :, cols],
+                    along(order[2], o),
+                )
+                for o in (1, 3, 2)
+            ]
 
     rescale = 1.0 / 2048
 
-    def finish(k, step, out):
-        p3 = pos[ORDERS[k][2]]
-        for c in step:
-            c.wait_recv()
-        total = F3[k, p3]
-        for o in range(3):
-            total = total + R3[k, o].astype(F32)
-        out[...] = total * rescale
-
-    skip1 = gradient(0, OG)
+    def finish(k, out):
+        for g, (order, start, width) in enumerate(GROUPS):
+            for c in steps[k, g, 4]:
+                c.wait_recv()
+            cols = pl.ds(start, 2 * width)
+            total = F3[k, pos[order[2]], :, cols]
+            for o in range(3):
+                total = total + R3[k, o, :, cols].astype(F32)
+            out[:, cols] = total * rescale
+
+    gradient(0, OG)
+    gradient(1, OG)
     backflow(theirs)
-    hg_copy = send(HG.at[core], HG.at[core], partner)
-    transposed(2, HG.at[core])
-    inner1 = gradient(2, S)
-    outer1 = gradient(1, OG)
-
-    bsend[0, :, pl.ds(0, HALF)] = jnp.sum(HG[core].astype(F32), axis=0, keepdims=True)
+    for g in range(3):
+        transposed(2, g, HG)
+    pass_on(0)
+    gradient(2, S)
+    pass_on(1)
+
+    bsend[0, :, pl.ds(0, HALF)] = jnp.sum(HG[...].astype(F32), axis=0, keepdims=True)
     bsend[0, :, pl.ds(HALF, D)] = jnp.sum(OG[...].astype(F32), axis=0, keepdims=True)
 
     def bias_send(i):
@@ -501,25 +530,28 @@
         bsend[i + 1] = bsend[i] + brecv[i, 0] + brecv[i, 1] + brecv[i, 2]
 
     bias1 = bias_send(0)
-    one_hot_sel(1 - core)
-    skip2 = pass_on(0, skip1)
-    isel_body(isel_send)
-    isel_copy = send(isel_send, isel.at[core], partner)
-    inner2 = pass_on(2, inner1)
-    hg_copy.wait_recv()
-    isel_copy.wait_recv()
-
-    def input_body(i, _):
-        rows = part(i, 256)
-        igf[:, rows] = (
-            mm(isel[0], HG[0, rows, :], NT)
-            + mm(isel[1], HG[1, rows, :], NT)
-            + mm(Ws[...], OG[rows, :], NT)
-        )
-        return 0
-
-    lax.fori_loop(0, CHIP // 256, input_body, 0)
-    ig_send[...] = igf[pl.ds(pl.multiple_of(other_hi * PAD, 128), SHARD), :].astype(BF16)
+    for i in range(CHIP // 256):
+        rows = pl.ds(i * 256, 256)
+        igp[:, rows] = mm(Wi[...], HG[rows, :], TT)
+    igp_copies = []
+    for j in range(2):
+        rows = pl.ds(pl.multiple_of(j * 640 + (1 - core) * SHARD, 64), SHARD)
+        igp_copies.append(send(igp.at[rows, :], igp_recv.at[j], partner))
+    second_phase(0)
+    pass_on(2)
+    for i in range(CHIP // 256):
+        rows = pl.ds(i * 256, 256)
+        igf[:, rows] = mm(Ws[...], OG[rows, :], NT)
+    for c in igp_copies:
+        c.wait_recv()
+
+    def columns(hi):
+        here = pl.ds(pl.multiple_of(hi * PAD, 128), SHARD)
+        there = pl.ds(pl.multiple_of(hi * 640 + core * SHARD, 64), SHARD)
+        return igf[here, :] + igp[there, :] + igp_recv[hi]
+
+    ig_send[...] = columns(other_hi).astype(BF16)
+    igf[own_rows, :] = columns(x_hi)
     lower, upper = pl.ds(0, SHARD // 2), pl.ds(SHARD // 2, SHARD // 2)
     ig1 = (
         send(ig_send.at[lower, :], ig_mid.at[lower, :], along("x", 1)),
@@ -529,33 +561,32 @@
         igf.at[own_rows, :], in_out.at[:, part(x_hi, CHIP)], lsem.at[len(loads)]
     )
     out0.start()
-    outer2 = pass_on(1, outer1)
+    second_phase(1)
     bias_add(0, bias1)
     bias2 = bias_send(1)
-    skip3 = second_phase(0, skip1, skip2)
+    pass_on_second(0)
+    second_phase(2)
+    pass_on_second(1)
+    third_phase(0)
     for c in ig1:
         c.wait_recv()
     ig2 = (
         send(ig_mid.at[lower, :], ig_recv.at[lower, :], along("x", 1)),
         send(ig_mid.at[upper, :], ig_recv.at[upper, :], along("x", 3)),
     )
-    inner3 = second_phase(2, inner1, inner2)
-    skip4 = pass_on_second(0, skip3)
-    outer3 = second_phase(1, outer1, outer2)
+    pass_on_second(2)
     bias_add(1, bias2)
     bias3 = bias_send(2)
-    inner4 = pass_on_second(2, inner3)
-    skip5 = third_phase(0, skip3, skip4)
-    outer4 = pass_on_second(1, outer3)
+    third_phase(1)
+    third_phase(2)
     for c in ig2:
         c.wait_recv()
-    outs[...] = ig_recv[...].astype(F32)
+    others = pl.ds(pl.multiple_of(other_hi * PAD, 128), SHARD)
+    igf[others, :] = ig_recv[...].astype(F32)
     out1 = pltpu.make_async_copy(
-        outs, in_out.at[:, part(other_hi, CHIP)], lsem.at[len(loads) + 1]
+        igf.at[others, :], in_out.at[:, part(other_hi, CHIP)], lsem.at[len(loads) + 1]
     )
     out1.start()
-    inner5 = third_phase(2, inner3, inner4)
-    outer5 = third_phase(1, outer3, outer4)
     bias_add(2, bias3)
 
     def pick(v, start):
@@ -570,16 +601,17 @@
 
     ib_out[...] = pick(bsend[3, :, pl.ds(0, HALF)], x_hi * PAD + dp * 10)[:, :10]
     ob_out[...] = pick(bsend[3, :, pl.ds(HALF, D)], dp * 40)[:, :40]
-    finish(0, skip5, gs_out)
-    finish(2, inner5, gi_out)
-    finish(1, outer5, go_out)
+    finish(0, gs_out)
+    finish(1, go_out)
+    finish(2, gi_out)
+    assert len(sent) == N_SENDS
     for c in sent:
         c.wait_send()
     out0.wait()
     out1.wait()
 
 
-N_SENDS = 136
+N_SENDS = 218
 
 
 def write_out(*refs):
@@ -625,13 +657,11 @@
             pltpu.VMEM((CORE, 128), F32),
             pltpu.VMEM((HALF, D), BF16),
             pltpu.VMEM((3, OWN, HALF), BF16),
-            pltpu.VMEM((2, HALF, HALF), BF16),
-            pltpu.VMEM((HALF, HALF), BF16),
             pltpu.VMEM((CHIP, HALF), BF16),
             pltpu.VMEM((CHIP, HALF), BF16),
             pltpu.VMEM((CHIP, HALF), F32),
-            pltpu.VMEM((3, OWN, CHIP), BF16),
-            pltpu.VMEM((2, CHIP, HALF), BF16),
+            pltpu.VMEM((3, 3, OWN, CHIP), BF16),
+            pltpu.VMEM((CHIP, HALF), BF16),
             pltpu.VMEM((CHIP, D), BF16),
             pltpu.VMEM((CORE, D), F32),
             pltpu.VMEM((1, D), F32),
@@ -656,17 +686,18 @@
             pltpu.VMEM((3, 3, C3, D), BF16),
             pltpu.VMEM((4, 1, HALF + D), F32),
             pltpu.VMEM((3, 3, 1, HALF + D), F32),
+            pltpu.VMEM((D, CHIP), F32),
+            pltpu.VMEM((2, SHARD, CHIP), F32),
             pltpu.VMEM((HALF, CHIP), F32),
             pltpu.VMEM((SHARD, CHIP), BF16),
             pltpu.VMEM((SHARD, CHIP), BF16),
             pltpu.VMEM((SHARD, CHIP), BF16),
-            pltpu.VMEM((SHARD, CHIP), F32),
             pltpu.SemaphoreType.DMA((8,)),
             pltpu.SemaphoreType.DMA((N_SENDS,)),
             pltpu.SemaphoreType.DMA((N_SENDS,)),
         ],
         compiler_params=pltpu.CompilerParams(
-            collective_id=0, has_side_effects=True, vmem_limit_bytes=60 * 1024 * 1024
+            collective_id=0, has_side_effects=True, vmem_limit_bytes=63 * 1024 * 1024
         ),
     )(series, wi, wo, ws, ib, ob, targets, levels, counts)
     input_grad, inner, outer, skip, inbias, outbias = pl.pallas_call(

time: 82.6 us -> 81.4 us (0.985)
  Pallas kernels: 81.8 us -> 80.4 us
    pallas_call x1, Pallas kernels: 79.5 us -> 78.1 us  [on_device(): pl.pallas_call(kernel, out_shape=shapes, in_specs=[hbm] * 4 + [vmem] * 2...]
where the time goes in v3:
time: 81.4 us; the launch traced here: 81.2 us
  Pallas kernels  80.4 us (99%)
    pallas_call x1, Pallas kernels, on_device(): pl.pallas_call(kernel, out_shape=shapes, in_specs=[hbm] * 4 + [vmem] * 2...  78.1 us
    pallas_call x1, Pallas kernels, on_device(): pl.pallas_call(write_out, out_shape=shapes, in_specs=[hbm] * 6, out_specs...  2.26 us

profile of v3, /device:TPU:0, one launch (start us, length us, event | category | flops | bytes accessed | tf_op | source)
XLA Modules:
  0.0 81.2 jit_solution(8868608247537449940)
XLA Ops:
  0.6 78.1 %shard_map.136 = (f32[320,1024]{1,0:T(8,128)}, f32[10,1280]{1,0:T(8,128)}, f32[10,1280]{1,0:T(8,128)}, f32[10,1280]{1,0:T(8,128)}, f32[1,10]{1,0:T(1,128)}, /*index=5*/f32[1,40]{1,0:T(1,128)}) custom-call(bf16[1024,1280]{1,0:T(8,128)(2,1)} %series_hbm.1, bf16[320,1280]{1,0:T(8,128)(2,1)} %wi_hbm.1, bf16[320,1280]{1,0:T(8,128)(2,1)} %wo_hbm.1, ...), custom_call_target="tpu_custom_call" | custom-call | tf_op jit(solution)/shard_map/pallas_call | solution.py:646
  78.8 2.3 %shard_map.137 = (f32[320,1024]{1,0:T(8,128)}, f32[10,1280]{1,0:T(8,128)}, f32[10,1280]{1,0:T(8,128)}, f32[10,1280]{1,0:T(8,128)}, f32[1,10]{1,0:T(1,128)}, /*index=5*/f32[1,40]{1,0:T(1,128)}) custom-call(f32[320,1024]{1,0:T(8,128)} %get-tuple-element.18.refs_0_, f32[10,1280]{1,0:T(8,128)} %get-tuple-element.19.refs_1_, ...), custom_call_target="tpu_custom_call" | custom-call | tf_op jit(solution)/shard_map/pallas_call | solution.py:703

commit v4 on v3

--- a/solution.py
+++ b/solution.py
@@ -271,6 +271,8 @@
         H[:, cols] = (pre * sig).astype(BF16)
         DV[:, cols] = sig * (1.0 + pre * (1.0 - sig))
         return 0
+
+    mine, theirs = part(core, CORE), part(1 - core, CORE)
 
     one_hot_sel(core)
     l_series.wait()
@@ -291,52 +293,55 @@
     relay(1, 0)
     l_t.wait()
     lax.fori_loop(0, 2, spread_body, 0)
-    forward_first(5)
+    forward_second(4)
     forward_second(2)
     relay(2, 0)
-    lax.fori_loop(2, 5, spread_body, 0)
+    lax.fori_loop(2, 4, spread_body, 0)
+    forward_first(5)
     forward_second(3)
     relay(3, 0)
+    forward_second(5)
     relay(0, 1)
-    transposed(0, 1, sH)
-    forward_second(4)
+    lax.fori_loop(4, 5, spread_body, 0)
     relay(4, 0)
     relay(1, 1)
-    forward_second(5)
+    transposed(0, 1, sH)
+    relay(2, 1)
     relay(5, 0)
-    relay(2, 1)
     transposed(0, 2, sH)
+    relay(3, 1)
     arrived(0)
     arrived(1)
     b_crossed.wait_recv()
-    relay(3, 1)
     lax.fori_loop(0, 2, hidden_body, 0, unroll=True)
     relay(4, 1)
     lax.fori_loop(2, 3, hidden_body, 0)
     relay(5, 1)
-    transposed(1, 0, H)
-    for i in range(2, 6):
-        arrived(i)
-
-    mine, theirs = part(core, CORE), part(1 - core, CORE)
-
-    def predict(rows, cols):
-        return mm(H[rows, :], Wo[:, cols]) + mm(sH[rows, :], Ws[:, cols])
+    arrived(2)
+    arrived(3)
+
+    def skip_body(i, _):
+        cols = part(i, 256)
+        p_send[i] = mm(sH[theirs, :], Ws[:, cols])
+        p_own[:, cols] = mm(sH[mine, :], Ws[:, cols])
+        return 0
+
+    lax.fori_loop(0, D // 256, skip_body, 0, unroll=True)
+    arrived(4)
+    arrived(5)
 
     p_copies = []
     for i in range(D // 256):
         cols = pl.ds(i * 256, 256)
-        p_send[i] = predict(theirs, cols)
+        p_send[i] = p_send[i] + mm(H[theirs, :], Wo[:, cols])
         p_copies.append(send(p_send.at[i], p_recv.at[i], partner))
 
     def predict_body(i, _):
         cols = part(i, 256)
-        p_own[:, cols] = predict(mine, cols)
+        p_own[:, cols] = p_own[:, cols] + mm(H[mine, :], Wo[:, cols])
         return 0
 
     lax.fori_loop(0, D // 256, predict_body, 0, unroll=True)
-    transposed(1, 1, H)
-    transposed(1, 2, H)
     for c in p_copies:
         c.wait_recv()
 
@@ -509,6 +514,8 @@
             out[:, cols] = total * rescale
 
     gradient(0, OG)
+    for g in range(3):
+        transposed(1, g, H)
     gradient(1, OG)
     backflow(theirs)
     for g in range(3):

time: 81.4 us -> 78.2 us (0.961)
  Pallas kernels: 80.4 us -> 77.2 us
    pallas_call x1, Pallas kernels: 78.1 us -> 74.9 us  [on_device(): pl.pallas_call(kernel, out_shape=shapes, in_specs=[hbm] * 4 + [vmem] * 2...]
where the time goes in v4:
time: 78.2 us; the launch traced here: 78 us
  Pallas kernels  77.2 us (99%)
  between operations  0.82 us (1%)
    pallas_call x1, Pallas kernels, on_device(): pl.pallas_call(kernel, out_shape=shapes, in_specs=[hbm] * 4 + [vmem] * 2...  74.9 us
    pallas_call x1, Pallas kernels, on_device(): pl.pallas_call(write_out, out_shape=shapes, in_specs=[hbm] * 6, out_specs...  2.26 us

profile of v4, /device:TPU:0, one launch (start us, length us, event | category | flops | bytes accessed | tf_op | source)
XLA Modules:
  0.0 78.0 jit_solution(3007834201534522090)
XLA Ops:
  0.6 74.9 %shard_map.136 = (f32[320,1024]{1,0:T(8,128)}, f32[10,1280]{1,0:T(8,128)}, f32[10,1280]{1,0:T(8,128)}, f32[10,1280]{1,0:T(8,128)}, f32[1,10]{1,0:T(1,128)}, /*index=5*/f32[1,40]{1,0:T(1,128)}) custom-call(bf16[1024,1280]{1,0:T(8,128)(2,1)} %series_hbm.1, bf16[320,1280]{1,0:T(8,128)(2,1)} %wi_hbm.1, bf16[320,1280]{1,0:T(8,128)(2,1)} %wo_hbm.1, ...), custom_call_target="tpu_custom_call" | custom-call | tf_op jit(solution)/shard_map/pallas_call | solution.py:653
  75.6 2.3 %shard_map.137 = (f32[320,1024]{1,0:T(8,128)}, f32[10,1280]{1,0:T(8,128)}, f32[10,1280]{1,0:T(8,128)}, f32[10,1280]{1,0:T(8,128)}, f32[1,10]{1,0:T(1,128)}, /*index=5*/f32[1,40]{1,0:T(1,128)}) custom-call(f32[320,1024]{1,0:T(8,128)} %get-tuple-element.18.refs_0_, f32[10,1280]{1,0:T(8,128)} %get-tuple-element.19.refs_1_, ...), custom_call_target="tpu_custom_call" | custom-call | tf_op jit(solution)/shard_map/pallas_call | solution.py:710

commit v5 on v4

--- a/solution.py
+++ b/solution.py
@@ -441,8 +441,11 @@
 
     steps = {}
 
-    def gradient(k, right):
+    def gradient(k, right, left=None):
         for g, (order, start, width) in enumerate(GROUPS):
+            if left is not None:
+                transposed(k, g, left)
+
             def body(i, _, g=g):
                 cols = part(i, 256)
                 value = mm(LT[k, g], right[:, cols])
@@ -498,7 +501,7 @@
                     ST3.at[k, rem(p3 + o, 4), :, cols], R3.at[k, o - 1, :, cols],
                     along(order[2], o),
                 )
-                for o in (1, 3, 2)
+                for o in (2, 1, 3)
             ]
 
     rescale = 1.0 / 2048
@@ -514,9 +517,7 @@
             out[:, cols] = total * rescale
 
     gradient(0, OG)
-    for g in range(3):
-        transposed(1, g, H)
-    gradient(1, OG)
+    gradient(1, OG, H)
     backflow(theirs)
     for g in range(3):
         transposed(2, g, HG)

time: 78.2 us -> 77.6 us (level)
  no operation moved by 1% of the time
where the time goes in v5:
time: 77.6 us; the launch traced here: 77.4 us
  Pallas kernels  76.6 us (99%)
  between operations  0.82 us (1%)
    pallas_call x1, Pallas kernels, on_device(): pl.pallas_call(kernel, out_shape=shapes, in_specs=[hbm] * 4 + [vmem] * 2...  74.3 us
    pallas_call x1, Pallas kernels, on_device(): pl.pallas_call(write_out, out_shape=shapes, in_specs=[hbm] * 6, out_specs...  2.26 us

profile of v5, /device:TPU:0, one launch (start us, length us, event | category | flops | bytes accessed | tf_op | source)
XLA Modules:
  0.0 77.4 jit_solution(6970302786401040586)
XLA Ops:
  0.6 74.3 %shard_map.136 = (f32[320,1024]{1,0:T(8,128)}, f32[10,1280]{1,0:T(8,128)}, f32[10,1280]{1,0:T(8,128)}, f32[10,1280]{1,0:T(8,128)}, f32[1,10]{1,0:T(1,128)}, /*index=5*/f32[1,40]{1,0:T(1,128)}) custom-call(bf16[1024,1280]{1,0:T(8,128)(2,1)} %series_hbm.1, bf16[320,1280]{1,0:T(8,128)(2,1)} %wi_hbm.1, bf16[320,1280]{1,0:T(8,128)(2,1)} %wo_hbm.1, ...), custom_call_target="tpu_custom_call" | custom-call | tf_op jit(solution)/shard_map/pallas_call | solution.py:654
  75.0 2.3 %shard_map.137 = (f32[320,1024]{1,0:T(8,128)}, f32[10,1280]{1,0:T(8,128)}, f32[10,1280]{1,0:T(8,128)}, f32[10,1280]{1,0:T(8,128)}, f32[1,10]{1,0:T(1,128)}, /*index=5*/f32[1,40]{1,0:T(1,128)}) custom-call(f32[320,1024]{1,0:T(8,128)} %get-tuple-element.18.refs_0_, f32[10,1280]{1,0:T(8,128)} %get-tuple-element.19.refs_1_, ...), custom_call_target="tpu_custom_call" | custom-call | tf_op jit(solution)/shard_map/pallas_call | solution.py:711
